TPU v7x, 32 devices: a 4x4x1 block of a 4x4x8 slice. The times are simulated.
32 devices in a mesh: grp: 1 (over z), comp: 4 (over y), row: 8 (over x, core).
Axes of the slice: x: 4, y: 4, z: 1, core: 2. Of those that a mesh axis runs over, the one named last changes fastest.
The devices are a block of a 4x4x8 slice.
Arguments:
- points: bfloat16 [2048, 256], P(('grp', 'row'))
- mu_init: float32 [2, 16384, 128], P(None, ('grp', 'comp'))
- logpi_init: float32 [2, 16384], P(None, ('grp', 'comp'))
- inv_temp: float32 [3], replicated
Outputs:
- output 1: float32 [2, 16384, 128], P(None, ('grp', 'comp'))
- output 2: float32 [2, 16384], P(None, ('grp', 'comp'))
- output 3: float32 [2, 2048], P(None, ('grp', 'row'))
All inputs are finite; a program needn't handle non-finite values.
Results may differ from a plain program's by a relative error of at most 0.00128443.
Values are sent between devices in bfloat16 or wider.
A program may use at most 768 MiB of HBM per device.

v0:
```python
import jax
import jax.numpy as jnp
from jax import lax
from jax.sharding import PartitionSpec as P

EPS_COUNT = 1e-6
PRIOR_ALPHA = 1e-3


def solution(mesh):
    comp_size = mesh.shape["comp"]
    row_size = mesh.shape["row"]

    def local_fit(x_local, mu_init, logpi_init, inv_temp):
        n_rows, full_dim = x_local.shape
        half_dim = full_dim // 2
        n_local = mu_init.shape[1]
        total_pts = n_rows * row_size
        total_comp = n_local * comp_size
        x_fits = jnp.transpose(x_local.reshape(n_rows, 2, half_dim), (1, 0, 2))
        sq_norm = jnp.sum(jnp.square(x_fits.astype(jnp.float32)), axis=2)
        mean_vecs = mu_init
        log_wts = logpi_init
        for sweep_idx in range(inv_temp.shape[0]):
            beta_t = inv_temp[sweep_idx]
            mu_sq = jnp.sum(mean_vecs * mean_vecs, axis=2)
            cross_dot = jnp.einsum("snh,skh->snk", x_fits, mean_vecs.astype(jnp.bfloat16), preferred_element_type=jnp.float32)
            logits = log_wts[:, None, :] - beta_t * (sq_norm[:, :, None] - 2.0 * cross_dot + mu_sq[:, None, :])
            row_max = lax.pmax(jnp.max(logits, axis=2), "comp")
            shifted = jnp.exp(logits - row_max[:, :, None])
            row_sum = lax.psum(jnp.sum(shifted, axis=2), "comp")
            log_norm = row_max + jnp.log(row_sum)
            resp_f = shifted / row_sum[:, :, None]
            counts = jnp.sum(resp_f, axis=1)
            stat_sum = jnp.einsum("snk,snh->skh", resp_f.astype(jnp.bfloat16), x_fits, preferred_element_type=jnp.float32)
            counts, stat_sum = lax.psum((counts, stat_sum), "row")
            mean_vecs = stat_sum / (counts[:, :, None] + EPS_COUNT)
            log_wts = jnp.log((counts + PRIOR_ALPHA) / (total_pts + total_comp * PRIOR_ALPHA))
        return mean_vecs, log_wts, log_norm

    return jax.shard_map(
        local_fit,
        mesh=mesh,
        in_specs=(P(("grp", "row"), None), P(None, ("grp", "comp"), None), P(None, ("grp", "comp")), P()),
        out_specs=(P(None, ("grp", "comp"), None), P(None, ("grp", "comp")), P(None, ("grp", "row"))),
        check_vma=False,
    )
```

profile of v0, /device:TPU:97, one launch (start us, length us, event | category | flops | bytes accessed | tf_op | source)
XLA Modules:
  0.0 344.3 jit_solution(2145926609938238478)
XLA Ops:
  12.2 7.6 %fusion.30 = (f32[2,256]{1,0:T(2,128)S(1)}, f32[2,256,4096]{2,1,0:T(8,128)}) fusion(f32[2,4096]{1,0:T(2,128)S(1)} %multiply_reduce_fusion.2, f32[2,4096,128]{2,1,0:T(8,128)} %param.5, f32[2,256]{1,0:T(2,128)S(1)} %multiply_reduce_fusion.3, f32[]{:T(128)} %bitcast, f32[2,4096]{1,0:T(2,128)} %param.6, bf16[256,256]{1,0:T(8,128)(2,1)S(1)} %copy-done), kind=kOutput, calls=%fused_computation.50 | convolution fusion | flops 550501888 | bytes 12783620 | tf_op jit(solution)/shard_map/snh,skh->snk/dot_general | solution.py:27
  19.7 11.2 %pmax.21 = f32[2,256]{1,0:T(2,128)S(1)} all-reduce(f32[2,256]{1,0:T(2,128)S(1)} %get-tuple-element.12), channel_id=1, replica_groups=mesh['grp'=1,'comp'=4,'row'=8] {'comp'}, use_global_device_ids=true, to_apply=%region_3.0 | all-reduce | flops 512 | bytes 4096 | tf_op jit(solution)/shard_map/pmax | solution.py:29
  30.9 4.6 %fusion.3 = f32[2,256]{1,0:T(2,128)S(1)} fusion(f32[2,256,4096]{2,1,0:T(8,128)} %get-tuple-element.13, f32[2,256]{1,0:T(2,128)S(1)} %pmax.21), kind=kLoop, calls=%fused_computation.11 | loop fusion | flops 4193792 | bytes 8392704 | tf_op jit(solution)/shard_map/reduce_sum | solution.py:31
  35.6 6.1 %psum.63 = f32[2,256]{1,0:T(2,128)S(1)} all-reduce(f32[2,256]{1,0:T(2,128)S(1)} %fusion.3), channel_id=1, replica_groups=mesh['grp'=1,'comp'=4,'row'=8] {'comp'}, use_global_device_ids=true, to_apply=%region_5.0 | all-reduce | flops 512 | bytes 4096 | tf_op jit(solution)/shard_map/psum | solution.py:31
  41.6 7.7 %fusion.12 = f32[2,4096,128]{2,1,0:T(8,128)} fusion(f32[2,256,4096]{2,1,0:T(8,128)} %get-tuple-element.13, f32[2,256]{1,0:T(2,128)S(1)} %psum.63, f32[2,256]{1,0:T(2,128)S(1)} %pmax.21, bf16[256,256]{1,0:T(8,128)(2,1)S(1)} %copy-done), kind=kOutput, calls=%fused_computation.22 | convolution fusion | flops 543162368 | bytes 12718080 | tf_op jit(solution)/shard_map/snk,snh->skh/dot_general | solution.py:35
  49.5 4.3 %fusion.19 = f32[2,4096]{1,0:T(2,128)S(1)} fusion(f32[2,256]{1,0:T(2,128)S(1)} %psum.63, f32[2,256,4096]{2,1,0:T(8,128)} %get-tuple-element.13, f32[2,256]{1,0:T(2,128)S(1)} %pmax.21), kind=kLoop, calls=%fused_computation.27 | loop fusion | flops 6283264 | bytes 8425472 | tf_op jit(solution)/shard_map/reduce_sum | solution.py:34
  53.9 25.1 %psum.64 = f32[2,4096]{1,0:T(2,128)S(1)} all-reduce(f32[2,4096]{1,0:T(2,128)S(1)} %fusion.19), channel_id=1, replica_groups=mesh['grp'=1,'comp'=4,'row'=8] {'row'}, use_global_device_ids=true, to_apply=%region_7.0 | all-reduce | flops 8192 | bytes 65536 | tf_op jit(solution)/shard_map/psum | solution.py:36
  79.1 40.1 %all-reduce.4.cloned.1.call-done = f32[2,4096,128]{2,1,0:T(8,128)} async-done(((f32[2,4096,128]{2,1,0:T(8,128)}), f32[2,4096,128]{2,1,0:T(8,128)}) %all-reduce.4.cloned.1.call-update) | async-done | bytes 4194320 | tf_op jit(solution)/shard_map/psum | solution.py:36
  123.2 8.1 %bitcast_reduce_fusion.1 = (f32[2,256]{1,0:T(2,128)S(1)}, f32[2,4096,256]{2,1,0:T(8,128)}) fusion(f32[2,4096]{1,0:T(2,128)S(1)} %multiply_reduce_fusion.1, f32[2,4096,128]{2,1,0:T(8,128)} %all-reduce.4.cloned.1.call-done, f32[2,4096]{1,0:T(2,128)S(1)} %get-tuple-element.7, f32[2,256]{1,0:T(2,128)S(1)} %multiply_reduce_fusion.3, f32[]{:T(128)} %bitcast.2, ...), kind=kOutput, calls=%fused_computation.4 | convolution fusion | flops 551550464 | bytes 12816388 | tf_op jit(solution)/shard_map/snh,skh->snk/dot_general | solution.py:27
  131.3 8.7 %pmax.22 = f32[2,256]{1,0:T(2,128)S(1)} all-reduce(f32[2,256]{1,0:T(2,128)S(1)} %get-tuple-element.14), channel_id=1, replica_groups=mesh['grp'=1,'comp'=4,'row'=8] {'comp'}, use_global_device_ids=true, to_apply=%region_11.0 | all-reduce | flops 512 | bytes 4096 | tf_op jit(solution)/shard_map/pmax | solution.py:29
  140.0 4.5 %fusion.5 = f32[2,256]{1,0:T(2,128)S(1)} fusion(f32[2,4096,256]{2,1,0:T(8,128)} %get-tuple-element.15, f32[2,256]{1,0:T(2,128)S(1)} %pmax.22), kind=kLoop, calls=%fused_computation.13 | loop fusion | flops 4193792 | bytes 8392704 | tf_op jit(solution)/shard_map/reduce_sum | solution.py:31
  144.4 6.3 %psum.66 = f32[2,256]{1,0:T(2,128)S(1)} all-reduce(f32[2,256]{1,0:T(2,128)S(1)} %fusion.5), channel_id=1, replica_groups=mesh['grp'=1,'comp'=4,'row'=8] {'comp'}, use_global_device_ids=true, to_apply=%region_13.0 | all-reduce | flops 512 | bytes 4096 | tf_op jit(solution)/shard_map/psum | solution.py:31
  150.7 6.8 %fusion.10 = f32[2,4096,128]{2,1,0:T(8,128)} fusion(f32[2,4096,256]{2,1,0:T(8,128)} %get-tuple-element.15, f32[2,256]{1,0:T(2,128)S(1)} %psum.66, f32[2,256]{1,0:T(2,128)S(1)} %pmax.22, bf16[256,256]{1,0:T(8,128)(2,1)S(1)} %copy-done), kind=kOutput, calls=%fused_computation.19 | convolution fusion | flops 543162368 | bytes 12718080 | tf_op jit(solution)/shard_map/snk,snh->skh/dot_general | solution.py:35
  157.6 4.3 %fusion.17 = f32[2,4096]{1,0:T(2,128)S(1)} fusion(f32[2,256]{1,0:T(2,128)S(1)} %psum.66, f32[2,256]{1,0:T(2,128)S(1)} %pmax.22, f32[2,4096,256]{2,1,0:T(8,128)} %get-tuple-element.15), kind=kLoop, calls=%fused_computation.26 | loop fusion | flops 6283264 | bytes 8425472 | tf_op jit(solution)/shard_map/reduce_sum | solution.py:34
  161.9 26.5 %psum.67 = f32[2,4096]{1,0:T(2,128)S(1)} all-reduce(f32[2,4096]{1,0:T(2,128)S(1)} %fusion.17), channel_id=1, replica_groups=mesh['grp'=1,'comp'=4,'row'=8] {'row'}, use_global_device_ids=true, to_apply=%region_15.0 | all-reduce | flops 8192 | bytes 65536 | tf_op jit(solution)/shard_map/psum | solution.py:36
  188.4 38.0 %all-reduce.6.cloned.1.call-done = f32[2,4096,128]{2,1,0:T(8,128)} async-done(((f32[2,4096,128]{2,1,0:T(8,128)}), f32[2,4096,128]{2,1,0:T(8,128)}) %all-reduce.6.cloned.1.call-update) | async-done | bytes 4194320 | tf_op jit(solution)/shard_map/psum | solution.py:36
  230.4 8.1 %bitcast_reduce_fusion = (f32[2,256]{1,0:T(2,128)S(1)}, f32[2,4096,256]{2,1,0:T(8,128)}) fusion(f32[2,4096]{1,0:T(2,128)S(1)} %multiply_reduce_fusion, f32[2,4096,128]{2,1,0:T(8,128)} %all-reduce.6.cloned.1.call-done, f32[2,4096]{1,0:T(2,128)S(1)} %get-tuple-element.5, f32[2,256]{1,0:T(2,128)S(1)} %multiply_reduce_fusion.3, f32[]{:T(128)} %bitcast.4, ...), kind=kOutput, calls=%fused_computation.1 | convolution fusion | flops 551550464 | bytes 12816388 | tf_op jit(solution)/shard_map/snh,skh->snk/dot_general | solution.py:27
  238.6 8.7 %pmax.23 = f32[2,256]{1,0:T(2,128)S(1)} all-reduce(f32[2,256]{1,0:T(2,128)S(1)} %get-tuple-element.16), channel_id=1, replica_groups=mesh['grp'=1,'comp'=4,'row'=8] {'comp'}, use_global_device_ids=true, to_apply=%region_19.0 | all-reduce | flops 512 | bytes 4096 | tf_op jit(solution)/shard_map/pmax | solution.py:29
  247.3 4.5 %fusion.7 = f32[2,256]{1,0:T(2,128)S(1)} fusion(f32[2,4096,256]{2,1,0:T(8,128)} %get-tuple-element.17, f32[2,256]{1,0:T(2,128)S(1)} %pmax.23), kind=kLoop, calls=%fused_computation.15 | loop fusion | flops 4193792 | bytes 8392704 | tf_op jit(solution)/shard_map/reduce_sum | solution.py:31
  251.7 6.1 %psum.69 = f32[2,256]{1,0:T(2,128)S(1)} all-reduce(f32[2,256]{1,0:T(2,128)S(1)} %fusion.7), channel_id=1, replica_groups=mesh['grp'=1,'comp'=4,'row'=8] {'comp'}, use_global_device_ids=true, to_apply=%region_21.0 | all-reduce | flops 512 | bytes 4096 | tf_op jit(solution)/shard_map/psum | solution.py:31
  257.8 6.8 %fusion.8 = f32[2,4096,128]{2,1,0:T(8,128)} fusion(f32[2,4096,256]{2,1,0:T(8,128)} %get-tuple-element.17, f32[2,256]{1,0:T(2,128)S(1)} %psum.69, f32[2,256]{1,0:T(2,128)S(1)} %pmax.23, bf16[256,256]{1,0:T(8,128)(2,1)S(1)} %copy-done), kind=kOutput, calls=%fused_computation.16 | convolution fusion | flops 543162368 | bytes 12718080 | tf_op jit(solution)/shard_map/snk,snh->skh/dot_general | solution.py:35
  264.7 4.3 %fusion.14 = f32[2,4096]{1,0:T(2,128)S(1)} fusion(f32[2,256]{1,0:T(2,128)S(1)} %psum.69, f32[2,256]{1,0:T(2,128)S(1)} %pmax.23, f32[2,4096,256]{2,1,0:T(8,128)} %get-tuple-element.17), kind=kLoop, calls=%fused_computation.25 | loop fusion | flops 6283264 | bytes 8425472 | tf_op jit(solution)/shard_map/reduce_sum | solution.py:34
  268.9 26.5 %psum.71 = f32[2,4096]{1,0:T(2,128)S(1)} all-reduce(f32[2,4096]{1,0:T(2,128)S(1)} %fusion.14), channel_id=1, replica_groups=mesh['grp'=1,'comp'=4,'row'=8] {'row'}, use_global_device_ids=true, to_apply=%region_24.0 | all-reduce | flops 8192 | bytes 65536 | tf_op jit(solution)/shard_map/psum | solution.py:36
  296.7 36.9 %all-reduce.8.cloned.1.call-done = f32[2,4096,128]{2,1,0:T(8,128)} async-done(((f32[2,4096,128]{2,1,0:T(8,128)}), f32[2,4096,128]{2,1,0:T(8,128)}) %all-reduce.8.cloned.1.call-update) | async-done | bytes 4194320 | tf_op jit(solution)/shard_map/psum | solution.py:36
  (18 shorter events, 18.7 us)
Async XLA Ops:
  7.2 1.5 copy-start
  7.2 112.0 %all-reduce.4.cloned.1.call-start = ((), (), s32[]{:S(2)}) async-start(), calls=%async_computation | async-start | bytes 8388608 | tf_op jit(solution)/shard_map/psum | solution.py:36
  49.4 177.0 %all-reduce.6.cloned.1.call-start = ((), (), s32[]{:S(2)}) async-start(), calls=%async_computation.1 | async-start | bytes 8388608 | tf_op jit(solution)/shard_map/psum | solution.py:36
  157.6 176.0 %all-reduce.8.cloned.1.call-start = ((), (), s32[]{:S(2)}) async-start(), calls=%async_computation.2 | async-start | bytes 8388608 | tf_op jit(solution)/shard_map/psum | solution.py:36
Sparse Core Ops, SparseCore 0:
  49.6 69.5 all-reduce.3
  157.7 68.7 all-reduce.5
  264.8 68.6 all-reduce.7
where the time goes:
time: 346 us; the launch traced here: 344 us
  blocking collectives  125 us (36%)
  waiting for transfers between devices  115 us (33%)
  matrix products  45.2 us (13%)
  other arithmetic  43.5 us (13%)
  between operations  13.8 us (4%)
    psum x3, waiting for transfers between devices, local_fit(): counts, stat_sum = lax.psum((counts, stat_sum), 'row')  115 us
    psum x3, blocking collectives, local_fit(): counts, stat_sum = lax.psum((counts, stat_sum), 'row')  78.1 us
    pmax x3, blocking collectives, local_fit(): row_max = lax.pmax(jnp.max(logits, axis=2), 'comp')  28.5 us
    dot_general x3, matrix products, local_fit(): jnp.einsum('snh,skh->snk', x_fits, mean_vecs.astype(jnp.bfloat16), prefer...  23.8 us
    dot_general x3, matrix products, local_fit(): jnp.einsum('snk,snh->skh', resp_f.astype(jnp.bfloat16), x_fits, preferred...  21.3 us
    psum x3, blocking collectives, local_fit(): row_sum = lax.psum(jnp.sum(shifted, axis=2), 'comp')  18.4 us
    reduce_sum x3, other arithmetic, local_fit(): row_sum = lax.psum(jnp.sum(shifted, axis=2), 'comp')  13.6 us
    reduce_sum x3, other arithmetic, local_fit(): counts = jnp.sum(resp_f, axis=1)  12.9 us
  transfers between devices with their start and end apart: 3, of which 3 were waited for; matrix products, arithmetic and copies ran while one was open for 4% of the time, Pallas kernels for 0%

commit v1 on v0

v1 whole, which is shorter than its diff:
```python
import functools
import math

import jax
import jax.numpy as jnp
from jax import lax
from jax.experimental import pallas as pl
from jax.experimental.pallas import tpu as pltpu
from jax.sharding import PartitionSpec as P

EPS_COUNT = 1e-6
PRIOR_ALPHA = 1e-3
LOG2E = math.log2(math.e)
LN2 = math.log(2.0)
LANES = 128
MESH = pl.DeviceIdType.MESH
NT = (((1,), (1,)), ((), ()))


def em_kernel(dims, beta_ref, x_ref, mu_hbm, logpi_ref, o_mu, o_small,
              xg, mu_f, mu_b, a_bc, lbuf, rb, s_acc, n_acc, mloc, stat_src, stat_buf,
              mu_all, small_src, small_buf,
              loc_sem, out_sem, x_send, x_recv, st_send, st_recv, sm_send, sm_recv,
              ag_send, ag_recv, sib_send, sib_recv):
    fits, n_comp, n_row, sweeps = dims["fits"], dims["comp"], dims["row"], dims["sweeps"]
    n_rows, half = x_ref.shape[0], mu_f.shape[1]
    nx = n_row // fits
    kd = mu_f.shape[0]
    cp = n_rows * fits
    lb = cp // LANES
    n_peer = n_comp * nx
    pieces = dims["pieces"]
    kp = kd // pieces
    total_pts = n_rows * n_row
    total_comp = kd * nx * n_comp

    grp = lax.axis_index("grp")
    comp = lax.axis_index("comp")
    row = lax.axis_index("row")
    fit = lax.rem(row, fits)
    xi = row // fits
    me = comp * nx + xi

    def dev(c, r):
        return (grp, c, r)

    def stat_peer(k):
        d_c, d_x = k // nx, k % nx
        return lax.rem(comp + d_c, n_comp), lax.rem(xi + d_x, nx)

    mu_cp = pltpu.make_async_copy(mu_hbm.at[fit, pl.ds(pl.multiple_of(xi * kd, kd), kd), :], mu_f, loc_sem)
    mu_cp.start()

    barrier = pltpu.get_barrier_semaphore()
    n_sig = 0
    for k in range(1, n_peer):
        c, x = stat_peer(k)
        pl.semaphore_signal(barrier, inc=1, device_id=dev(c, x * fits + fit), device_id_type=MESH)
        n_sig += 1
    for k in range(nx):
        for f in range(1, fits):
            x = lax.rem(xi + k, nx)
            pl.semaphore_signal(barrier, inc=1, device_id=dev(comp, x * fits + lax.rem(fit + f, fits)), device_id_type=MESH)
            n_sig += 1
    pl.semaphore_wait(barrier, n_sig)

    def x_cols(f):
        return pl.ds(pl.multiple_of(f * half, half), half)

    my_rows = pl.ds(pl.multiple_of(fit * n_rows, n_rows), n_rows)
    x_copies = []
    for k in (0, 1, 3, 2) if nx == 4 else range(nx):
        for f in range(fits):
            if k == 0 and f == 0:
                continue
            x = lax.rem(xi + k, nx)
            ft = lax.rem(fit + f, fits)
            cpy = pltpu.make_async_remote_copy(
                src_ref=x_ref.at[:, x_cols(ft)],
                dst_ref=xg.at[xi, my_rows],
                send_sem=x_send, recv_sem=x_recv.at[xi],
                device_id=dev(comp, x * fits + ft), device_id_type=MESH)
            cpy.start()
            x_copies.append(cpy)
    xg[xi, my_rows, :] = x_ref[:, x_cols(fit)]

    def comp_terms(t, rows, mu, logw):
        beta = beta_ref[t]
        sq = jnp.sum(mu * mu, axis=1, keepdims=True)
        a = (logw - beta * sq) * LOG2E
        a_bc[rows, :] = jnp.broadcast_to(a, (a.shape[0], LANES))
        mu_b[rows, :] = mu.astype(jnp.bfloat16)

    mu_cp.wait()
    for b in range(kd // LANES):
        rows = pl.ds(b * LANES, LANES)
        lw = logpi_ref[:, pl.ds(pl.multiple_of(xi * kd + b * LANES, LANES), LANES)]
        pick = lax.broadcasted_iota(jnp.int32, (fits, LANES), 0) == fit
        lw = jnp.sum(jnp.where(pick, lw, 0.0), axis=0, keepdims=True)
        lw = jnp.transpose(jnp.broadcast_to(lw, (LANES, LANES)))
        comp_terms(0, rows, mu_f[rows, :], lw[:, 0:1])

    def lanes_tile(v):
        return jnp.concatenate([v] * lb, axis=1)

    KB = 128
    nkb = kd // KB

    def e_chunk(t, q):
        c2 = beta_ref[t] * (2.0 * LOG2E)
        lbuf[q] = lax.dot_general(mu_b[...], xg[q], NT, preferred_element_type=jnp.float32)

        def pass1(b, m8):
            rows = pl.ds(pl.multiple_of(b * KB, KB), KB)
            l = lbuf[q, rows, :] * c2 + lanes_tile(a_bc[rows, :])
            lbuf[q, rows, :] = l
            return jnp.maximum(m8, jnp.max(l.reshape(KB // 8, 8, cp), axis=0))

        m8 = lax.fori_loop(0, nkb, pass1, jnp.full((8, cp), -jnp.inf, jnp.float32))
        m = jnp.max(m8, axis=0, keepdims=True)

        def pass2(b, r8):
            rows = pl.ds(pl.multiple_of(b * KB, KB), KB)
            p = jnp.exp2(lbuf[q, rows, :] - m)
            lbuf[q, rows, :] = p
            return r8 + jnp.sum(p.reshape(KB // 8, 8, cp), axis=0)

        r8 = lax.fori_loop(0, nkb, pass2, jnp.zeros((8, cp), jnp.float32))
        r = jnp.sum(r8, axis=0, keepdims=True)
        for j in range(lb):
            cols = slice(j * LANES, (j + 1) * LANES)
            for ref in (stat_src.at[t, q], stat_buf.at[t, q, me]):
                ref[0, j:j + 1, :] = m[:, cols]
                ref[1, j:j + 1, :] = r[:, cols]

    def stat_copy(t, q, k):
        c, x = stat_peer(k)
        return pltpu.make_async_remote_copy(
            src_ref=stat_src.at[t, q], dst_ref=stat_buf.at[t, q, me],
            send_sem=st_send.at[t, q], recv_sem=st_recv.at[t, q],
            device_id=dev(c, x * fits + fit), device_id_type=MESH)

    def stat_start(t, q):
        for k in range(1, n_peer):
            stat_copy(t, q, k).start()

    def stat_wait(t, q, send):
        part = stat_buf.at[t, q, pl.ds(0, n_peer - 1)]
        d = pltpu.make_async_copy(part, part, st_send.at[t, q] if send else st_recv.at[t, q])
        d.wait()

    def scale_of(t, q):
        m_all = stat_buf[t, q, :, 0]
        r_all = stat_buf[t, q, :, 1]
        m = jnp.max(m_all, axis=0)
        r = jnp.sum(r_all * jnp.exp2(m_all - m), axis=0)
        return m, r, jnp.exp2(stat_src[t, q, 0] - m) / r

    def m_rows(q, rows, nrow, sc):
        sc_row = jnp.concatenate([jnp.broadcast_to(sc[j:j + 1, :], (nrow, LANES)) for j in range(lb)], axis=1)
        res = lbuf[q, rows, :] * sc_row
        cnt = res[:, 0:LANES]
        for j in range(1, lb):
            cnt = cnt + res[:, j * LANES:(j + 1) * LANES]
        rb[rows, :] = res.astype(jnp.bfloat16)
        return cnt

    def m_chunk(t, q, first):
        m, r, sc = scale_of(t, q)

        def body(b, carry):
            rows = pl.ds(pl.multiple_of(b * KB, KB), KB)
            cnt = m_rows(q, rows, KB, sc)
            n_acc[rows, :] = jnp.where(first, cnt, n_acc[rows, :] + cnt)
            return carry

        lax.fori_loop(0, nkb, body, 0)
        s = jnp.dot(rb[...], xg[q], preferred_element_type=jnp.float32)
        s_acc[...] = jnp.where(first, s, s_acc[...] + s)
        return m, r

    order = (0, 1, 3, 2) if nx == 4 else tuple(range(nx))
    for off in order:
        q = lax.rem(xi + off, nx)
        n_in = (fits - 1) if off == 0 else fits
        part = xg.at[q, pl.ds(0, n_in * n_rows)]
        pltpu.make_async_copy(part, part, x_recv.at[q]).wait()
        e_chunk(0, q)
        stat_start(0, q)

    def sweep(t, carry):
        def m_body(q, c):
            stat_wait(t, q, False)
            m_chunk(t, q, q == 0)
            return c

        lax.fori_loop(0, nx, m_body, 0)

        def terms(b, c):
            rows = pl.ds(pl.multiple_of(b * KB, KB), KB)
            cnt = jnp.sum(n_acc[rows, :], axis=1, keepdims=True)
            mu = s_acc[rows, :] / (cnt + EPS_COUNT)
            logw = jnp.log((cnt + PRIOR_ALPHA) / (total_pts + total_comp * PRIOR_ALPHA))
            comp_terms(t + 1, rows, mu, logw)
            return c

        lax.fori_loop(0, nkb, terms, 0)

        def e_body(q, c):
            e_chunk(t + 1, q)
            stat_start(t + 1, q)
            return c

        lax.fori_loop(0, nx, e_body, 0)
        return carry

    lax.fori_loop(0, sweeps - 1, sweep, 0)

    tl = sweeps - 1

    sq_rows = []
    for j in range(lb):
        xb = xg[xi, j * LANES:(j + 1) * LANES, :].astype(jnp.float32)
        sq_rows.append(jnp.sum(jnp.transpose(xb * xb), axis=0, keepdims=True))
    sq = jnp.concatenate(sq_rows, axis=0)

    def m_last(q, c):
        stat_wait(tl, q, False)
        m, r = m_chunk(tl, q, q == 0)
        return c

    lax.fori_loop(0, nx, m_last, 0)
    m, r, _ = scale_of(tl, xi)
    small_src[1, 0:lb, :] = m * LN2 + jnp.log(r) - beta_ref[tl] * sq

    right = lax.rem(xi + 1, nx)
    left = lax.rem(xi + nx - 1, nx)
    far = lax.rem(xi + 2, nx)
    sib = xi * fits + lax.rem(fit + 1, fits)

    def span(x, p):
        return pl.ds(pl.multiple_of(x * kd + p * kp, kp), kp)

    def mu_copy(x, p, send_sem, recv_sem, r):
        part = mu_all.at[fit, span(x, p)]
        return pltpu.make_async_remote_copy(src_ref=part, dst_ref=part, send_sem=send_sem, recv_sem=recv_sem,
                                            device_id=dev(comp, r), device_id_type=MESH)

    def out_copy(f, x, p):
        return pltpu.make_async_copy(mu_all.at[f, span(x, p)], o_mu.at[f, span(x, p)], out_sem)

    waits = []
    half_p = pieces // 2
    porder = [p // 2 + (p % 2) * half_p for p in range(pieces)]
    for p in porder:
        for b in range(kp // LANES):
            rows = pl.ds(p * kp + b * LANES, LANES)
            na = n_acc[rows, :]
            cnt = jnp.sum(na, axis=1, keepdims=True)
            mu_all[fit, pl.ds(pl.multiple_of(xi * kd + p * kp + b * LANES, LANES), LANES), :] = s_acc[rows, :] / (cnt + EPS_COUNT)
            n_row_v = jnp.sum(jnp.transpose(na), axis=0, keepdims=True)
            j = p * (kp // LANES) + b
            small_src[0, j:j + 1, :] = jnp.log((n_row_v + PRIOR_ALPHA) / (total_pts + total_comp * PRIOR_ALPHA))
        to_r = mu_copy(xi, p, ag_send.at[0, p], ag_recv.at[0, p], right * fits + fit)
        to_l = mu_copy(xi, p, ag_send.at[1, p], ag_recv.at[1, p], left * fits + fit)
        to_s = mu_copy(xi, p, sib_send.at[0, p], sib_recv.at[0, p], sib)
        to_r.start()
        to_l.start()
        to_s.start()
        oc = out_copy(fit, xi, p)
        oc.start()
        waits += [to_r.wait_send, to_l.wait_send, to_s.wait_send, oc.wait]

    sm_me = small_buf.at[row]
    sm_copies = []
    for k in range(1, n_row):
        r = lax.rem(row + k, n_row)
        cpy = pltpu.make_async_remote_copy(src_ref=small_src, dst_ref=sm_me, send_sem=sm_send, recv_sem=sm_recv,
                                           device_id=dev(comp, r), device_id_type=MESH)
        cpy.start()
        sm_copies.append(cpy)
    small_buf[row] = small_src[...]

    for i, p in enumerate(porder):
        for side, src in ((0, left), (1, right)):
            mu_copy(src, p, ag_send.at[2, p], ag_recv.at[side, p], sib).wait_recv()
            if (p < half_p) == (side == 0):
                fw = mu_copy(src, p, ag_send.at[2, p], ag_recv.at[2, p],
                             (right if side == 0 else left) * fits + fit)
                fw.start()
                waits.append(fw.wait_send)
            d = 1 if side == 0 else 3
            ts = mu_copy(src, p, sib_send.at[d, p], sib_recv.at[d, p], sib)
            ts.start()
            oc = out_copy(fit, src, p)
            oc.start()
            waits += [ts.wait_send, oc.wait]
    for p in porder:
        mu_copy(far, p, ag_send.at[2, p], ag_recv.at[2, p], sib).wait_recv()
        ts = mu_copy(far, p, sib_send.at[2, p], sib_recv.at[2, p], sib)
        ts.start()
        oc = out_copy(fit, far, p)
        oc.start()
        waits += [ts.wait_send, oc.wait]
    ofit = lax.rem(fit + 1, fits)
    for d, src in ((0, xi), (1, left), (3, right), (2, far)):
        for p in porder:
            part = mu_all.at[ofit, span(src, p)]
            pltpu.make_async_copy(part, part, sib_recv.at[d, p]).wait()
            oc = out_copy(ofit, src, p)
            oc.start()
            waits.append(oc.wait)

    part = small_buf.at[pl.ds(0, n_row - 1)]
    pltpu.make_async_copy(part, part, sm_recv).wait()
    pltpu.make_async_copy(part, part, sm_send).wait()
    o_small[...] = small_buf[...]
    for w in waits:
        w()
    def drain(t, c):
        for q in range(nx):
            stat_wait(t, q, True)
        return c
    lax.fori_loop(0, sweeps, drain, 0)
    for cpy in x_copies:
        cpy.wait_send()


def solution(mesh):
    comp_size = mesh.shape["comp"]
    row_size = mesh.shape["row"]

    def local_fit(x_local, mu_init, logpi_init, inv_temp):
        n_rows, full_dim = x_local.shape
        fits, n_local, half = mu_init.shape
        sweeps = inv_temp.shape[0]
        nx = row_size // fits
        kd = n_local // nx
        cp = n_rows * fits
        n_peer = comp_size * nx
        pieces = 4
        dims = {"fits": fits, "comp": comp_size, "row": row_size, "sweeps": sweeps, "pieces": pieces}
        f32, bf16 = jnp.float32, jnp.bfloat16
        dma = pltpu.SemaphoreType.DMA
        srows = cp // LANES
        mu, small = pl.pallas_call(
            functools.partial(em_kernel, dims),
            out_shape=(jax.ShapeDtypeStruct((fits, n_local, half), f32),
                       jax.ShapeDtypeStruct((row_size, 2, kd // LANES, LANES), f32)),
            in_specs=[pl.BlockSpec(memory_space=pltpu.SMEM),
                      pl.BlockSpec(memory_space=pltpu.VMEM),
                      pl.BlockSpec(memory_space=pl.ANY),
                      pl.BlockSpec(memory_space=pltpu.VMEM)],
            out_specs=(pl.BlockSpec(memory_space=pl.ANY),
                       pl.BlockSpec(memory_space=pltpu.VMEM)),
            scratch_shapes=[
                pltpu.VMEM((nx, cp, half), bf16),
                pltpu.VMEM((kd, half), f32),
                pltpu.VMEM((kd, half), bf16),
                pltpu.VMEM((kd, LANES), f32),
                pltpu.VMEM((nx, kd, cp), f32),
                pltpu.VMEM((kd, cp), bf16),
                pltpu.VMEM((kd, half), f32),
                pltpu.VMEM((kd, LANES), f32),
                pltpu.VMEM((8, LANES), f32),
                pltpu.VMEM((sweeps, nx, 2, srows, LANES), f32),
                pltpu.VMEM((sweeps, nx, n_peer, 2, srows, LANES), f32),
                pltpu.VMEM((fits, n_local, half), f32),
                pltpu.VMEM((2, kd // LANES, LANES), f32),
                pltpu.VMEM((row_size, 2, kd // LANES, LANES), f32),
                dma, dma, dma, dma((nx,)),
                dma((sweeps, nx)), dma((sweeps, nx)),
                dma, dma,
                dma((3, pieces)), dma((3, pieces)), dma((4, pieces)), dma((4, pieces)),
            ],
            compiler_params=pltpu.CompilerParams(collective_id=0, has_side_effects=True,
                                                 vmem_limit_bytes=60 * 1024 * 1024),
        )(inv_temp, x_local, mu_init, logpi_init)
        row = lax.axis_index("row")
        xi = row // fits
        small = small.reshape(nx, fits, 2, kd // LANES, LANES)
        log_wts = jnp.transpose(small[:, :, 0], (1, 0, 2, 3)).reshape(fits, n_local)
        own = lax.dynamic_index_in_dim(small, xi, 0, keepdims=False)[:, 1]
        per = n_rows // LANES
        lse = lax.dynamic_slice_in_dim(own, lax.rem(row, fits) * per, per, 1).reshape(fits, n_rows)
        return mu, log_wts, lse

    return jax.shard_map(
        local_fit,
        mesh=mesh,
        in_specs=(P(("grp", "row"), None), P(None, ("grp", "comp"), None), P(None, ("grp", "comp")), P()),
        out_specs=(P(None, ("grp", "comp"), None), P(None, ("grp", "comp")), P(None, ("grp", "row"))),
        check_vma=False,
    )
```

time: 346 us -> 80.6 us (0.23)
  blocking collectives: 125 us -> 0 us
  waiting for transfers between devices: 115 us -> 0 us
  Pallas kernels: 0 us -> 72.5 us
  matrix products: 45.2 us -> 0 us
  other arithmetic: 43.5 us -> 0 us
  between operations: 13.8 us -> 0.66 us
  local copies, waits for them, and re-layouts: 1.39 us -> 7.19 us
    psum x3 -> x0, waiting for transfers between devices: 115 us -> none  [local_fit(): counts, stat_sum = lax.psum((counts, stat_sum), 'row')]
    psum x6 -> x0, blocking collectives: 96.5 us -> none  [the longest x3 78.1 us: local_fit(): counts, stat_sum = lax.psum((counts, stat_sum), 'row')]
    pallas_call x0 -> x1, Pallas kernels: none -> 72.5 us  [local_fit(): pl.pallas_call(functools.partial(em_kernel, dims), out_shape=(jax.ShapeDt...]
    dot_general x6 -> x0, matrix products: 45.2 us -> none  [the longest x3 23.8 us: local_fit(): jnp.einsum('snh,skh->snk', x_fits, mean_vecs.astype(jnp.bfloat16), prefer...]
    reduce_sum x10 -> x0, other arithmetic: 37.9 us -> none  [the longest x3 13.6 us: local_fit(): row_sum = lax.psum(jnp.sum(shifted, axis=2), 'comp')]
    pmax x3 -> x0, blocking collectives: 28.5 us -> none  [local_fit(): row_max = lax.pmax(jnp.max(logits, axis=2), 'comp')]
    unnamed x2 -> x5, local copies, waits for them, and re-layouts: 0.01 us -> 6.46 us
    div x1 -> x0, other arithmetic: 4.22 us -> none  [local_fit(): mean_vecs = stat_sum / (counts[:, :, None] + EPS_COUNT)]
  transfers between devices with their start and end apart: 3 -> 0, of which waited for: 3 -> 0; matrix products, arithmetic and copies ran while one was open for 4% -> 0% of each run, Pallas kernels for 0% -> 0%
where the time goes in v1:
time: 80.6 us; the launch traced here: 80.3 us
  Pallas kernels  72.5 us (90%)
  local copies, waits for them, and re-layouts  7.19 us (9%)
    pallas_call x1, Pallas kernels, local_fit(): pl.pallas_call(functools.partial(em_kernel, dims), out_shape=(jax.ShapeDt...  72.5 us
    unnamed x5, local copies, waits for them, and re-layouts  6.46 us

profile of v1, /device:TPU:97, one launch (start us, length us, event | category | flops | bytes accessed | tf_op | source)
XLA Modules:
  0.0 80.3 jit_solution(9935343572336709272)
XLA Ops:
  0.7 72.5 %shard_map.67 = (f32[2,4096,128]{2,1,0:T(8,128)}, f32[8,2,8,128]{3,2,1,0:T(8,128)}) custom-call(f32[3]{0:T(128)} %beta_ref.1, bf16[256,256]{1,0:T(8,128)(2,1)} %x_ref.1, f32[2,4096,128]{2,1,0:T(8,128)} %mu_hbm.1, f32[2,4096]{1,0:T(2,128)} %logpi_ref.1), custom_call_target="tpu_custom_call" | custom-call | tf_op jit(solution)/shard_map/pallas_call | solution.py:346
  73.1 0.7 dynamic-slice_bitcast_fusion
  73.9 0.6 copy.15
  74.5 0.8 copy_bitcast_fusion.1
  75.2 0.6 copy.14
  75.9 4.5 %copy.17 = f32[2,4096,128]{2,1,0:T(8,128)} copy(f32[2,4096,128]{2,1,0:T(8,128)} %get-tuple-element.10) | data formatting | bytes 8388608
  (2 shorter events, 0.0 us)

commit v2 on v1

--- a/solution.py
+++ b/solution.py
@@ -17,10 +17,10 @@
 NT = (((1,), (1,)), ((), ()))
 
 
-def em_kernel(dims, beta_ref, x_ref, mu_hbm, logpi_ref, o_mu, o_small,
-              xg, mu_f, mu_b, a_bc, lbuf, rb, s_acc, n_acc, mloc, stat_src, stat_buf,
-              mu_all, small_src, small_buf,
-              loc_sem, out_sem, x_send, x_recv, st_send, st_recv, sm_send, sm_recv,
+def em_kernel(dims, beta_hbm, x_hbm, mu_hbm, logpi_hbm, mu_all, small_buf,
+              beta_ref, x_ref, logpi_ref, xg, mu_f, mu_b, a_bc, lbuf, rb, s_acc, n_acc,
+              stat_src, stat_buf, small_src,
+              loc_sem, x_send, x_recv, st_send, st_recv, sm_send, sm_recv,
               ag_send, ag_recv, sib_send, sib_recv):
     fits, n_comp, n_row, sweeps = dims["fits"], dims["comp"], dims["row"], dims["sweeps"]
     n_rows, half = x_ref.shape[0], mu_f.shape[1]
@@ -48,9 +48,6 @@
         d_c, d_x = k // nx, k % nx
         return lax.rem(comp + d_c, n_comp), lax.rem(xi + d_x, nx)
 
-    mu_cp = pltpu.make_async_copy(mu_hbm.at[fit, pl.ds(pl.multiple_of(xi * kd, kd), kd), :], mu_f, loc_sem)
-    mu_cp.start()
-
     barrier = pltpu.get_barrier_semaphore()
     n_sig = 0
     for k in range(1, n_peer):
@@ -62,7 +59,33 @@
             x = lax.rem(xi + k, nx)
             pl.semaphore_signal(barrier, inc=1, device_id=dev(comp, x * fits + lax.rem(fit + f, fits)), device_id_type=MESH)
             n_sig += 1
-    pl.semaphore_wait(barrier, n_sig)
+
+    loads = [pltpu.make_async_copy(x_hbm, x_ref, loc_sem.at[0]),
+             pltpu.make_async_copy(mu_hbm.at[fit, pl.ds(pl.multiple_of(xi * kd, kd), kd), :], mu_f, loc_sem.at[1]),
+             pltpu.make_async_copy(logpi_hbm, logpi_ref, loc_sem.at[2]),
+             pltpu.make_async_copy(beta_hbm, beta_ref, loc_sem.at[3])]
+    for cpy in loads:
+        cpy.start()
+
+    def comp_terms(t, rows, mu, logw):
+        beta = beta_ref[t]
+        sq = jnp.sum(mu * mu, axis=1, keepdims=True)
+        a = (logw - beta * sq) * LOG2E
+        a_bc[rows, :] = jnp.broadcast_to(a, (a.shape[0], LANES))
+        mu_b[rows, :] = mu.astype(jnp.bfloat16)
+
+    for cpy in loads:
+        cpy.wait()
+    for b in range(kd // LANES):
+        rows = pl.ds(b * LANES, LANES)
+        lw = logpi_ref[:, pl.ds(pl.multiple_of(xi * kd + b * LANES, LANES), LANES)]
+        pick = lax.broadcasted_iota(jnp.int32, (fits, LANES), 0) == fit
+        lw = jnp.sum(jnp.where(pick, lw, 0.0), axis=0, keepdims=True)
+        lw = jnp.transpose(jnp.broadcast_to(lw, (LANES, LANES)))
+        comp_terms(0, rows, mu_f[rows, :], lw[:, 0:1])
+
+    with jax.named_scope("bar"):
+        pl.semaphore_wait(barrier, n_sig)
 
     def x_cols(f):
         return pl.ds(pl.multiple_of(f * half, half), half)
@@ -84,48 +107,31 @@
             x_copies.append(cpy)
     xg[xi, my_rows, :] = x_ref[:, x_cols(fit)]
 
-    def comp_terms(t, rows, mu, logw):
-        beta = beta_ref[t]
-        sq = jnp.sum(mu * mu, axis=1, keepdims=True)
-        a = (logw - beta * sq) * LOG2E
-        a_bc[rows, :] = jnp.broadcast_to(a, (a.shape[0], LANES))
-        mu_b[rows, :] = mu.astype(jnp.bfloat16)
-
-    mu_cp.wait()
-    for b in range(kd // LANES):
-        rows = pl.ds(b * LANES, LANES)
-        lw = logpi_ref[:, pl.ds(pl.multiple_of(xi * kd + b * LANES, LANES), LANES)]
-        pick = lax.broadcasted_iota(jnp.int32, (fits, LANES), 0) == fit
-        lw = jnp.sum(jnp.where(pick, lw, 0.0), axis=0, keepdims=True)
-        lw = jnp.transpose(jnp.broadcast_to(lw, (LANES, LANES)))
-        comp_terms(0, rows, mu_f[rows, :], lw[:, 0:1])
-
     def lanes_tile(v):
         return jnp.concatenate([v] * lb, axis=1)
 
     KB = 128
     nkb = kd // KB
 
-    def e_chunk(t, q):
+    def e_dot(q):
+        with jax.named_scope("edot"):
+            lbuf[q] = lax.dot_general(mu_b[...], xg[q], NT, preferred_element_type=jnp.float32)
+
+    def e_soft(t, q):
         c2 = beta_ref[t] * (2.0 * LOG2E)
-        lbuf[q] = lax.dot_general(mu_b[...], xg[q], NT, preferred_element_type=jnp.float32)
-
-        def pass1(b, m8):
-            rows = pl.ds(pl.multiple_of(b * KB, KB), KB)
+        m8 = jnp.full((8, cp), -jnp.inf, jnp.float32)
+        for b in range(nkb):
+            rows = slice(b * KB, (b + 1) * KB)
             l = lbuf[q, rows, :] * c2 + lanes_tile(a_bc[rows, :])
             lbuf[q, rows, :] = l
-            return jnp.maximum(m8, jnp.max(l.reshape(KB // 8, 8, cp), axis=0))
-
-        m8 = lax.fori_loop(0, nkb, pass1, jnp.full((8, cp), -jnp.inf, jnp.float32))
+            m8 = jnp.maximum(m8, jnp.max(l.reshape(KB // 8, 8, cp), axis=0))
         m = jnp.max(m8, axis=0, keepdims=True)
-
-        def pass2(b, r8):
-            rows = pl.ds(pl.multiple_of(b * KB, KB), KB)
+        r8 = jnp.zeros((8, cp), jnp.float32)
+        for b in range(nkb):
+            rows = slice(b * KB, (b + 1) * KB)
             p = jnp.exp2(lbuf[q, rows, :] - m)
             lbuf[q, rows, :] = p
-            return r8 + jnp.sum(p.reshape(KB // 8, 8, cp), axis=0)
-
-        r8 = lax.fori_loop(0, nkb, pass2, jnp.zeros((8, cp), jnp.float32))
+            r8 = r8 + jnp.sum(p.reshape(KB // 8, 8, cp), axis=0)
         r = jnp.sum(r8, axis=0, keepdims=True)
         for j in range(lb):
             cols = slice(j * LANES, (j + 1) * LANES)
@@ -147,7 +153,8 @@
     def stat_wait(t, q, send):
         part = stat_buf.at[t, q, pl.ds(0, n_peer - 1)]
         d = pltpu.make_async_copy(part, part, st_send.at[t, q] if send else st_recv.at[t, q])
-        d.wait()
+        with jax.named_scope("stwait"):
+            d.wait()
 
     def scale_of(t, q):
         m_all = stat_buf[t, q, :, 0]
@@ -167,16 +174,13 @@
 
     def m_chunk(t, q, first):
         m, r, sc = scale_of(t, q)
-
-        def body(b, carry):
-            rows = pl.ds(pl.multiple_of(b * KB, KB), KB)
-            cnt = m_rows(q, rows, KB, sc)
-            n_acc[rows, :] = jnp.where(first, cnt, n_acc[rows, :] + cnt)
-            return carry
-
-        lax.fori_loop(0, nkb, body, 0)
-        s = jnp.dot(rb[...], xg[q], preferred_element_type=jnp.float32)
-        s_acc[...] = jnp.where(first, s, s_acc[...] + s)
+        with jax.named_scope("mchunk"):
+            for b in range(nkb):
+                rows = slice(b * KB, (b + 1) * KB)
+                cnt = m_rows(q, rows, KB, sc)
+                n_acc[rows, :] = jnp.where(first, cnt, n_acc[rows, :] + cnt)
+            s = jnp.dot(rb[...], xg[q], preferred_element_type=jnp.float32)
+            s_acc[...] = jnp.where(first, s, s_acc[...] + s)
         return m, r
 
     order = (0, 1, 3, 2) if nx == 4 else tuple(range(nx))
@@ -184,8 +188,11 @@
         q = lax.rem(xi + off, nx)
         n_in = (fits - 1) if off == 0 else fits
         part = xg.at[q, pl.ds(0, n_in * n_rows)]
-        pltpu.make_async_copy(part, part, x_recv.at[q]).wait()
-        e_chunk(0, q)
+        with jax.named_scope("xwait"):
+            pltpu.make_async_copy(part, part, x_recv.at[q]).wait()
+        e_dot(q)
+        with jax.named_scope("esoft"):
+            e_soft(0, q)
         stat_start(0, q)
 
     def sweep(t, carry):
@@ -196,22 +203,28 @@
 
         lax.fori_loop(0, nx, m_body, 0)
 
-        def terms(b, c):
-            rows = pl.ds(pl.multiple_of(b * KB, KB), KB)
-            cnt = jnp.sum(n_acc[rows, :], axis=1, keepdims=True)
-            mu = s_acc[rows, :] / (cnt + EPS_COUNT)
-            logw = jnp.log((cnt + PRIOR_ALPHA) / (total_pts + total_comp * PRIOR_ALPHA))
-            comp_terms(t + 1, rows, mu, logw)
+        with jax.named_scope("terms"):
+            for b in range(nkb):
+                rows = slice(b * KB, (b + 1) * KB)
+                cnt = jnp.sum(n_acc[rows, :], axis=1, keepdims=True)
+                mu = s_acc[rows, :] / (cnt + EPS_COUNT)
+                logw = jnp.log((cnt + PRIOR_ALPHA) / (total_pts + total_comp * PRIOR_ALPHA))
+                comp_terms(t + 1, rows, mu, logw)
+        e_dot(0)
+
+        def e_body(q, c):
+            e_dot(q + 1)
+            with jax.named_scope("esoft"):
+                e_soft(t + 1, q)
+            with jax.named_scope("stsend"):
+                stat_start(t + 1, q)
             return c
 
-        lax.fori_loop(0, nkb, terms, 0)
-
-        def e_body(q, c):
-            e_chunk(t + 1, q)
-            stat_start(t + 1, q)
-            return c
-
-        lax.fori_loop(0, nx, e_body, 0)
+        lax.fori_loop(0, nx - 1, e_body, 0)
+        with jax.named_scope("esoft"):
+            e_soft(t + 1, nx - 1)
+        with jax.named_scope("stsend"):
+            stat_start(t + 1, nx - 1)
         return carry
 
     lax.fori_loop(0, sweeps - 1, sweep, 0)
@@ -245,9 +258,6 @@
         part = mu_all.at[fit, span(x, p)]
         return pltpu.make_async_remote_copy(src_ref=part, dst_ref=part, send_sem=send_sem, recv_sem=recv_sem,
                                             device_id=dev(comp, r), device_id_type=MESH)
-
-    def out_copy(f, x, p):
-        return pltpu.make_async_copy(mu_all.at[f, span(x, p)], o_mu.at[f, span(x, p)], out_sem)
 
     waits = []
     half_p = pieces // 2
@@ -267,9 +277,7 @@
         to_r.start()
         to_l.start()
         to_s.start()
-        oc = out_copy(fit, xi, p)
-        oc.start()
-        waits += [to_r.wait_send, to_l.wait_send, to_s.wait_send, oc.wait]
+        waits += [to_r.wait_send, to_l.wait_send, to_s.wait_send]
 
     sm_me = small_buf.at[row]
     sm_copies = []
@@ -292,29 +300,21 @@
             d = 1 if side == 0 else 3
             ts = mu_copy(src, p, sib_send.at[d, p], sib_recv.at[d, p], sib)
             ts.start()
-            oc = out_copy(fit, src, p)
-            oc.start()
-            waits += [ts.wait_send, oc.wait]
+            waits.append(ts.wait_send)
     for p in porder:
         mu_copy(far, p, ag_send.at[2, p], ag_recv.at[2, p], sib).wait_recv()
         ts = mu_copy(far, p, sib_send.at[2, p], sib_recv.at[2, p], sib)
         ts.start()
-        oc = out_copy(fit, far, p)
-        oc.start()
-        waits += [ts.wait_send, oc.wait]
+        waits.append(ts.wait_send)
     ofit = lax.rem(fit + 1, fits)
     for d, src in ((0, xi), (1, left), (3, right), (2, far)):
         for p in porder:
             part = mu_all.at[ofit, span(src, p)]
             pltpu.make_async_copy(part, part, sib_recv.at[d, p]).wait()
-            oc = out_copy(ofit, src, p)
-            oc.start()
-            waits.append(oc.wait)
 
     part = small_buf.at[pl.ds(0, n_row - 1)]
     pltpu.make_async_copy(part, part, sm_recv).wait()
     pltpu.make_async_copy(part, part, sm_send).wait()
-    o_small[...] = small_buf[...]
     for w in waits:
         w()
     def drain(t, c):
@@ -324,6 +324,29 @@
     lax.fori_loop(0, sweeps, drain, 0)
     for cpy in x_copies:
         cpy.wait_send()
+
+
+def finish_kernel(fits, mu_all, small, o_mu, o_logpi, o_lse, sem):
+    cp = pltpu.make_async_copy(mu_all, o_mu, sem)
+    cp.start()
+    row = lax.axis_index("row")
+    fit = lax.rem(row, fits)
+    first = row - fit
+    n_row, _, srows, _ = small.shape
+    nx = n_row // fits
+    kd = o_logpi.shape[1] // nx
+    n_rows = o_lse.shape[1]
+    per = n_rows // LANES
+    for f in range(fits):
+        for x in range(nx):
+            for j in range(kd // LANES):
+                o_logpi[f:f + 1, x * kd + j * LANES:x * kd + (j + 1) * LANES] = small[x * fits + f, 0, j:j + 1, :]
+        for j in range(per):
+            v = small[first + f, 1, j:j + 1, :]
+            for g in range(1, fits):
+                v = jnp.where(fit == g, small[first + f, 1, g * per + j:g * per + j + 1, :], v)
+            o_lse[f:f + 1, j * LANES:(j + 1) * LANES] = v
+    cp.wait()
 
 
 def solution(mesh):
@@ -343,17 +366,18 @@
         f32, bf16 = jnp.float32, jnp.bfloat16
         dma = pltpu.SemaphoreType.DMA
         srows = cp // LANES
+        hbm = pl.BlockSpec(memory_space=pltpu.HBM)
+        vmem = pl.BlockSpec(memory_space=pltpu.VMEM)
         mu, small = pl.pallas_call(
             functools.partial(em_kernel, dims),
-            out_shape=(jax.ShapeDtypeStruct((fits, n_local, half), f32),
-                       jax.ShapeDtypeStruct((row_size, 2, kd // LANES, LANES), f32)),
-            in_specs=[pl.BlockSpec(memory_space=pltpu.SMEM),
-                      pl.BlockSpec(memory_space=pltpu.VMEM),
-                      pl.BlockSpec(memory_space=pl.ANY),
-                      pl.BlockSpec(memory_space=pltpu.VMEM)],
-            out_specs=(pl.BlockSpec(memory_space=pl.ANY),
-                       pl.BlockSpec(memory_space=pltpu.VMEM)),
+            out_shape=(pltpu.VMEM((fits, n_local, half), f32),
+                       pltpu.VMEM((row_size, 2, kd // LANES, LANES), f32)),
+            in_specs=[hbm] * 4,
+            out_specs=(vmem, vmem),
             scratch_shapes=[
+                pltpu.SMEM((sweeps,), f32),
+                pltpu.VMEM((n_rows, full_dim), bf16),
+                pltpu.VMEM((fits, n_local), f32),
                 pltpu.VMEM((nx, cp, half), bf16),
                 pltpu.VMEM((kd, half), f32),
                 pltpu.VMEM((kd, half), bf16),
@@ -362,28 +386,27 @@
                 pltpu.VMEM((kd, cp), bf16),
                 pltpu.VMEM((kd, half), f32),
                 pltpu.VMEM((kd, LANES), f32),
-                pltpu.VMEM((8, LANES), f32),
                 pltpu.VMEM((sweeps, nx, 2, srows, LANES), f32),
                 pltpu.VMEM((sweeps, nx, n_peer, 2, srows, LANES), f32),
-                pltpu.VMEM((fits, n_local, half), f32),
                 pltpu.VMEM((2, kd // LANES, LANES), f32),
-                pltpu.VMEM((row_size, 2, kd // LANES, LANES), f32),
-                dma, dma, dma, dma((nx,)),
+                dma((4,)), dma, dma((nx,)),
                 dma((sweeps, nx)), dma((sweeps, nx)),
                 dma, dma,
                 dma((3, pieces)), dma((3, pieces)), dma((4, pieces)), dma((4, pieces)),
             ],
             compiler_params=pltpu.CompilerParams(collective_id=0, has_side_effects=True,
-                                                 vmem_limit_bytes=60 * 1024 * 1024),
-        )(inv_temp, x_local, mu_init, logpi_init)
-        row = lax.axis_index("row")
-        xi = row // fits
-        small = small.reshape(nx, fits, 2, kd // LANES, LANES)
-        log_wts = jnp.transpose(small[:, :, 0], (1, 0, 2, 3)).reshape(fits, n_local)
-        own = lax.dynamic_index_in_dim(small, xi, 0, keepdims=False)[:, 1]
-        per = n_rows // LANES
-        lse = lax.dynamic_slice_in_dim(own, lax.rem(row, fits) * per, per, 1).reshape(fits, n_rows)
-        return mu, log_wts, lse
+                                                 vmem_limit_bytes=48 * 1024 * 1024),
+        )(*[pltpu.with_memory_space_constraint(v, pltpu.HBM) for v in (inv_temp, x_local, mu_init, logpi_init)])
+        return pl.pallas_call(
+            functools.partial(finish_kernel, fits),
+            out_shape=(jax.ShapeDtypeStruct((fits, n_local, half), f32),
+                       jax.ShapeDtypeStruct((fits, n_local), f32),
+                       jax.ShapeDtypeStruct((fits, n_rows), f32)),
+            in_specs=[pl.BlockSpec(memory_space=pl.ANY), vmem],
+            out_specs=(hbm, vmem, vmem),
+            scratch_shapes=[dma],
+            compiler_params=pltpu.CompilerParams(vmem_limit_bytes=8 * 1024 * 1024),
+        )(pltpu.with_memory_space_constraint(mu, pltpu.VMEM), pltpu.with_memory_space_constraint(small, pltpu.VMEM))
 
     return jax.shard_map(
         local_fit,

time: 80.6 us -> 65.9 us (0.82)
  Pallas kernels: 72.5 us -> 65.1 us
  local copies, waits for them, and re-layouts: 7.19 us -> 0 us
    pallas_call x1 -> x2, Pallas kernels: 72.5 us -> 65.1 us  [the longest x1 62.5 us: local_fit(): pl.pallas_call(functools.partial(em_kernel, dims), out_shape=(pltpu.VMEM(...]
    unnamed x5 -> x0, local copies, waits for them, and re-layouts: 6.46 us -> none
where the time goes in v2:
time: 65.9 us; the launch traced here: 65.8 us
  Pallas kernels  65.1 us (99%)
    pallas_call x1, Pallas kernels, local_fit(): pl.pallas_call(functools.partial(em_kernel, dims), out_shape=(pltpu.VMEM(...  62.5 us
    pallas_call x1, Pallas kernels, local_fit(): pl.pallas_call(functools.partial(finish_kernel, fits), out_shape=(jax.Sha...  2.64 us

profile of v2, /device:TPU:97, one launch (start us, length us, event | category | flops | bytes accessed | tf_op | source)
XLA Modules:
  0.0 65.8 jit_solution(18170087816391635002)
XLA Ops:
  0.6 62.5 %shard_map.67 = (f32[2,4096,128]{2,1,0:T(8,128)S(1)}, f32[8,2,8,128]{3,2,1,0:T(8,128)S(1)}) custom-call(f32[3]{0:T(128)} %beta_hbm.1, bf16[256,256]{1,0:T(8,128)(2,1)} %x_hbm.1, f32[2,4096,128]{2,1,0:T(8,128)} %mu_hbm.1, f32[2,4096]{1,0:T(2,128)} %logpi_hbm.1), custom_call_target="tpu_custom_call" | custom-call | tf_op jit(solution)/shard_map/pallas_call | solution.py:371
  63.1 2.6 %shard_map.68 = (f32[2,4096,128]{2,1,0:T(8,128)}, f32[2,4096]{1,0:T(2,128)}, f32[2,256]{1,0:T(2,128)}) custom-call(f32[2,4096,128]{2,1,0:T(8,128)S(1)} %get-tuple-element.5.mu_all, f32[8,2,8,128]{3,2,1,0:T(8,128)S(1)} %get-tuple-element.6.small), custom_call_target="tpu_custom_call" | custom-call | tf_op jit(solution)/shard_map/pallas_call | solution.py:400

commit v3 on v2

--- a/solution.py
+++ b/solution.py
@@ -19,9 +19,9 @@
 
 def em_kernel(dims, beta_hbm, x_hbm, mu_hbm, logpi_hbm, mu_all, small_buf,
               beta_ref, x_ref, logpi_ref, xg, mu_f, mu_b, a_bc, lbuf, rb, s_acc, n_acc,
-              stat_src, stat_buf, small_src,
+              stat_src, stat_buf, small_src, a_row, xm_b, xa_row, xa_bc, xbuf, xrb, xs_acc, xn_acc,
               loc_sem, x_send, x_recv, st_send, st_recv, sm_send, sm_recv,
-              ag_send, ag_recv, sib_send, sib_recv):
+              bk_send, bk_recv, ar_send, ar_recv, far_send, far_recv, sib_send, sib_recv):
     fits, n_comp, n_row, sweeps = dims["fits"], dims["comp"], dims["row"], dims["sweeps"]
     n_rows, half = x_ref.shape[0], mu_f.shape[1]
     nx = n_row // fits
@@ -29,8 +29,6 @@
     cp = n_rows * fits
     lb = cp // LANES
     n_peer = n_comp * nx
-    pieces = dims["pieces"]
-    kp = kd // pieces
     total_pts = n_rows * n_row
     total_comp = kd * nx * n_comp
 
@@ -156,12 +154,19 @@
         with jax.named_scope("stwait"):
             d.wait()
 
-    def scale_of(t, q):
+    def totals_of(t, q):
         m_all = stat_buf[t, q, :, 0]
         r_all = stat_buf[t, q, :, 1]
         m = jnp.max(m_all, axis=0)
         r = jnp.sum(r_all * jnp.exp2(m_all - m), axis=0)
+        return m, r
+
+    def scale_of(t, q):
+        m, r = totals_of(t, q)
         return m, r, jnp.exp2(stat_src[t, q, 0] - m) / r
+
+    def lane_rows(v, nrow):
+        return jnp.concatenate([jnp.broadcast_to(v[j:j + 1, :], (nrow, LANES)) for j in range(lb)], axis=1)
 
     def m_rows(q, rows, nrow, sc):
         sc_row = jnp.concatenate([jnp.broadcast_to(sc[j:j + 1, :], (nrow, LANES)) for j in range(lb)], axis=1)
@@ -195,14 +200,31 @@
             e_soft(0, q)
         stat_start(0, q)
 
-    def sweep(t, carry):
+    right = lax.rem(xi + 1, nx)
+    left = lax.rem(xi + nx - 1, nx)
+    far = lax.rem(xi + 2, nx)
+    sides = ((0, right), (1, left))
+
+    def bulk_piece(p, width):
+        for d, x in sides:
+            rows = pl.ds(p * KB, width * KB)
+            pltpu.make_async_remote_copy(
+                src_ref=mu_b.at[rows], dst_ref=xm_b.at[d, rows],
+                send_sem=bk_send.at[d], recv_sem=bk_recv.at[d],
+                device_id=dev(comp, x * fits + fit), device_id_type=MESH).start()
+
+    def a_copy(d, x):
+        return pltpu.make_async_remote_copy(
+            src_ref=a_row, dst_ref=xa_row.at[d], send_sem=ar_send.at[d], recv_sem=ar_recv.at[d],
+            device_id=dev(comp, x * fits + fit), device_id_type=MESH)
+
+    def sweep(t, last):
         def m_body(q, c):
             stat_wait(t, q, False)
             m_chunk(t, q, q == 0)
             return c
 
         lax.fori_loop(0, nx, m_body, 0)
-
         with jax.named_scope("terms"):
             for b in range(nkb):
                 rows = slice(b * KB, (b + 1) * KB)
@@ -210,7 +232,13 @@
                 mu = s_acc[rows, :] / (cnt + EPS_COUNT)
                 logw = jnp.log((cnt + PRIOR_ALPHA) / (total_pts + total_comp * PRIOR_ALPHA))
                 comp_terms(t + 1, rows, mu, logw)
+                if last:
+                    a_row[b:b + 1, :] = jnp.transpose(a_bc[rows, :])[0:1, :]
         e_dot(0)
+        if last:
+            bulk_piece(0, 2)
+            for d, x in sides:
+                a_copy(d, x).start()
 
         def e_body(q, c):
             e_dot(q + 1)
@@ -218,6 +246,8 @@
                 e_soft(t + 1, q)
             with jax.named_scope("stsend"):
                 stat_start(t + 1, q)
+                if last:
+                    bulk_piece(q + 2, 1)
             return c
 
         lax.fori_loop(0, nx - 1, e_body, 0)
@@ -225,9 +255,15 @@
             e_soft(t + 1, nx - 1)
         with jax.named_scope("stsend"):
             stat_start(t + 1, nx - 1)
-        return carry
-
-    lax.fori_loop(0, sweeps - 1, sweep, 0)
+            if last:
+                bulk_piece(nx + 1, nkb - nx - 1)
+
+    def sweep_body(t, c):
+        sweep(t, False)
+        return c
+
+    lax.fori_loop(0, sweeps - 2, sweep_body, 0)
+    sweep(sweeps - 2, True)
 
     tl = sweeps - 1
 
@@ -237,80 +273,133 @@
         sq_rows.append(jnp.sum(jnp.transpose(xb * xb), axis=0, keepdims=True))
     sq = jnp.concatenate(sq_rows, axis=0)
 
-    def m_last(q, c):
-        stat_wait(tl, q, False)
-        m, r = m_chunk(tl, q, q == 0)
-        return c
-
-    lax.fori_loop(0, nx, m_last, 0)
-    m, r, _ = scale_of(tl, xi)
-    small_src[1, 0:lb, :] = m * LN2 + jnp.log(r) - beta_ref[tl] * sq
-
-    right = lax.rem(xi + 1, nx)
-    left = lax.rem(xi + nx - 1, nx)
-    far = lax.rem(xi + 2, nx)
+    kh = kd // 2
+    nh = kh // KB
+    c2_last = beta_ref[tl] * (2.0 * LOG2E)
     sib = xi * fits + lax.rem(fit + 1, fits)
-
-    def span(x, p):
-        return pl.ds(pl.multiple_of(x * kd + p * kp, kp), kp)
-
-    def mu_copy(x, p, send_sem, recv_sem, r):
-        part = mu_all.at[fit, span(x, p)]
-        return pltpu.make_async_remote_copy(src_ref=part, dst_ref=part, send_sem=send_sem, recv_sem=recv_sem,
-                                            device_id=dev(comp, r), device_id_type=MESH)
+    with jax.named_scope("bulkwait"):
+        for d in range(2):
+            pltpu.make_async_copy(xm_b.at[d], xm_b.at[d], bk_recv.at[d]).wait()
+            pltpu.make_async_copy(xa_row.at[d], xa_row.at[d], ar_recv.at[d]).wait()
+    with jax.named_scope("xterms"):
+        for d in range(2):
+            for b in range(nkb):
+                xa_bc[d, b * KB:(b + 1) * KB, :] = jnp.transpose(jnp.broadcast_to(xa_row[d, b:b + 1, :], (KB, LANES)))
+
+    owner = (comp * nx + left, comp * nx + right)
+
+    def x_units(q, first, halves):
+        m, r = totals_of(tl, q)
+        for d, h in enumerate(halves):
+            hrows = slice(h * kh, (h + 1) * kh)
+            xbuf[d] = lax.dot_general(xm_b[d, hrows, :], xg[q], NT, preferred_element_type=jnp.float32)
+        for d, h in enumerate(halves):
+            m_j = stat_buf[tl, q, owner[d], 0]
+            m_row = lane_rows(m_j, KB)
+            sc_row = lane_rows(jnp.exp2(m_j - m) / r, KB)
+            for b in range(nh):
+                rows = slice(b * KB, (b + 1) * KB)
+                grows = slice(h * kh + b * KB, h * kh + (b + 1) * KB)
+                l = xbuf[d, rows, :] * c2_last + lanes_tile(xa_bc[d, grows, :])
+                res = jnp.exp2(l - m_row) * sc_row
+                cnt = res[:, 0:LANES]
+                for j in range(1, lb):
+                    cnt = cnt + res[:, j * LANES:(j + 1) * LANES]
+                xrb[d, rows, :] = res.astype(jnp.bfloat16)
+                xn_acc[d, rows, :] = jnp.where(first, cnt, xn_acc[d, rows, :] + cnt)
+        for d, h in enumerate(halves):
+            s = jnp.dot(xrb[d], xg[q], preferred_element_type=jnp.float32)
+            xs_acc[d] = jnp.where(first, s, xs_acc[d] + s)
+
+    def mean_rows(na, sa):
+        return sa / (jnp.sum(na, axis=1, keepdims=True) + EPS_COUNT)
+
+    def span(x, start, size):
+        return pl.ds(pl.multiple_of(x * kd + start, KB), size)
 
     waits = []
-    half_p = pieces // 2
-    porder = [p // 2 + (p % 2) * half_p for p in range(pieces)]
-    for p in porder:
-        for b in range(kp // LANES):
-            rows = pl.ds(p * kp + b * LANES, LANES)
-            na = n_acc[rows, :]
-            cnt = jnp.sum(na, axis=1, keepdims=True)
-            mu_all[fit, pl.ds(pl.multiple_of(xi * kd + p * kp + b * LANES, LANES), LANES), :] = s_acc[rows, :] / (cnt + EPS_COUNT)
-            n_row_v = jnp.sum(jnp.transpose(na), axis=0, keepdims=True)
-            j = p * (kp // LANES) + b
-            small_src[0, j:j + 1, :] = jnp.log((n_row_v + PRIOR_ALPHA) / (total_pts + total_comp * PRIOR_ALPHA))
-        to_r = mu_copy(xi, p, ag_send.at[0, p], ag_recv.at[0, p], right * fits + fit)
-        to_l = mu_copy(xi, p, ag_send.at[1, p], ag_recv.at[1, p], left * fits + fit)
-        to_s = mu_copy(xi, p, sib_send.at[0, p], sib_recv.at[0, p], sib)
-        to_r.start()
-        to_l.start()
-        to_s.start()
-        waits += [to_r.wait_send, to_l.wait_send, to_s.wait_send]
-
-    sm_me = small_buf.at[row]
-    sm_copies = []
-    for k in range(1, n_row):
-        r = lax.rem(row + k, n_row)
-        cpy = pltpu.make_async_remote_copy(src_ref=small_src, dst_ref=sm_me, send_sem=sm_send, recv_sem=sm_recv,
+
+    def push(x, start, size, send_sem, recv_sem, r):
+        part = mu_all.at[fit, span(x, start, size)]
+        cpy = pltpu.make_async_remote_copy(src_ref=part, dst_ref=part, send_sem=send_sem, recv_sem=recv_sem,
                                            device_id=dev(comp, r), device_id_type=MESH)
         cpy.start()
-        sm_copies.append(cpy)
-    small_buf[row] = small_src[...]
-
-    for i, p in enumerate(porder):
-        for side, src in ((0, left), (1, right)):
-            mu_copy(src, p, ag_send.at[2, p], ag_recv.at[side, p], sib).wait_recv()
-            if (p < half_p) == (side == 0):
-                fw = mu_copy(src, p, ag_send.at[2, p], ag_recv.at[2, p],
-                             (right if side == 0 else left) * fits + fit)
-                fw.start()
-                waits.append(fw.wait_send)
-            d = 1 if side == 0 else 3
-            ts = mu_copy(src, p, sib_send.at[d, p], sib_recv.at[d, p], sib)
-            ts.start()
-            waits.append(ts.wait_send)
-    for p in porder:
-        mu_copy(far, p, ag_send.at[2, p], ag_recv.at[2, p], sib).wait_recv()
-        ts = mu_copy(far, p, sib_send.at[2, p], sib_recv.at[2, p], sib)
-        ts.start()
-        waits.append(ts.wait_send)
+        waits.append(cpy.wait_send)
+
+    def x_finish(d, h, b):
+        x = (left, right)[d]
+        rows = slice(b * KB, (b + 1) * KB)
+        mu_all[fit, span(x, h * kh + b * KB, KB), :] = mean_rows(xn_acc[d, rows, :], xs_acc[d, rows, :])
+
+    def xa_body(q, c):
+        stat_wait(tl, q, False)
+        with jax.named_scope("xunitA"):
+            x_units(q, q == 0, (0, 1))
+        return c
+
+    lax.fori_loop(0, nx, xa_body, 0)
+    with jax.named_scope("xfinA"):
+        for b in range(nh):
+            for d, x in sides:
+                x_finish(d, d, b)
+                push((left, right)[d], d * kh + b * KB, KB, far_send.at[d, b], far_recv.at[d, b], x * fits + fit)
+        for d in range(2):
+            push((left, right)[d], d * kh, kh, sib_send.at[d], sib_recv.at[d], sib)
+
+    def m_last(q, c):
+        m_chunk(tl, q, q == 0)
+        return c
+
+    lax.fori_loop(0, nx, m_last, 0)
+    with jax.named_scope("ownfin"):
+        m, r, _ = scale_of(tl, xi)
+        small_src[1, 0:lb, :] = m * LN2 + jnp.log(r) - beta_ref[tl] * sq
+        for b in range(nkb):
+            rows = slice(b * KB, (b + 1) * KB)
+            na = n_acc[rows, :]
+            mu_all[fit, span(xi, b * KB, KB), :] = mean_rows(na, s_acc[rows, :])
+            n_row_v = jnp.sum(jnp.transpose(na), axis=0, keepdims=True)
+            small_src[0, b:b + 1, :] = jnp.log((n_row_v + PRIOR_ALPHA) / (total_pts + total_comp * PRIOR_ALPHA))
+        push(xi, 0, kd, sib_send.at[2], sib_recv.at[2], sib)
+        for k in range(1, n_row):
+            r = lax.rem(row + k, n_row)
+            cpy = pltpu.make_async_remote_copy(src_ref=small_src, dst_ref=small_buf.at[row], send_sem=sm_send, recv_sem=sm_recv,
+                                               device_id=dev(comp, r), device_id_type=MESH)
+            cpy.start()
+        small_buf[row] = small_src[...]
+
+    def xb_body(q, c):
+        with jax.named_scope("xunitB"):
+            x_units(q, q == 0, (1, 0))
+        return c
+
+    lax.fori_loop(0, nx, xb_body, 0)
+    with jax.named_scope("xfinB"):
+        for d in range(2):
+            for b in range(nh):
+                x_finish(d, 1 - d, b)
+            push((left, right)[d], (1 - d) * kh, kh, sib_send.at[3 + d], sib_recv.at[3 + d], sib)
+
+    with jax.named_scope("farwait"):
+        for b in range(nh):
+            for d in range(2):
+                part = mu_all.at[fit, span(far, d * kh + b * KB, KB)]
+                pltpu.make_async_copy(part, part, far_recv.at[d, b]).wait()
+                k = 5 + d * nh + b
+                push(far, d * kh + b * KB, KB, sib_send.at[k], sib_recv.at[k], sib)
     ofit = lax.rem(fit + 1, fits)
-    for d, src in ((0, xi), (1, left), (3, right), (2, far)):
-        for p in porder:
-            part = mu_all.at[ofit, span(src, p)]
-            pltpu.make_async_copy(part, part, sib_recv.at[d, p]).wait()
+
+    def sib_wait(x, start, size, k):
+        part = mu_all.at[ofit, span(x, start, size)]
+        pltpu.make_async_copy(part, part, sib_recv.at[k]).wait()
+
+    with jax.named_scope("sibwait"):
+        sib_wait(xi, 0, kd, 2)
+        for d, x in ((0, left), (1, right)):
+            sib_wait(x, d * kh, kh, d)
+            sib_wait(x, (1 - d) * kh, kh, 3 + d)
+            for b in range(nh):
+                sib_wait(far, d * kh + b * KB, KB, 5 + d * nh + b)
 
     part = small_buf.at[pl.ds(0, n_row - 1)]
     pltpu.make_async_copy(part, part, sm_recv).wait()
@@ -324,6 +413,9 @@
     lax.fori_loop(0, sweeps, drain, 0)
     for cpy in x_copies:
         cpy.wait_send()
+    for d in range(2):
+        pltpu.make_async_copy(xm_b.at[d], xm_b.at[d], bk_send.at[d]).wait()
+        pltpu.make_async_copy(xa_row.at[d], xa_row.at[d], ar_send.at[d]).wait()
 
 
 def finish_kernel(fits, mu_all, small, o_mu, o_logpi, o_lse, sem):
@@ -361,8 +453,9 @@
         kd = n_local // nx
         cp = n_rows * fits
         n_peer = comp_size * nx
-        pieces = 4
-        dims = {"fits": fits, "comp": comp_size, "row": row_size, "sweeps": sweeps, "pieces": pieces}
+        kb = LANES
+        nh = kd // 2 // kb
+        dims = {"fits": fits, "comp": comp_size, "row": row_size, "sweeps": sweeps}
         f32, bf16 = jnp.float32, jnp.bfloat16
         dma = pltpu.SemaphoreType.DMA
         srows = cp // LANES
@@ -389,10 +482,19 @@
                 pltpu.VMEM((sweeps, nx, 2, srows, LANES), f32),
                 pltpu.VMEM((sweeps, nx, n_peer, 2, srows, LANES), f32),
                 pltpu.VMEM((2, kd // LANES, LANES), f32),
+                pltpu.VMEM((kd // LANES, LANES), f32),
+                pltpu.VMEM((2, kd, half), bf16),
+                pltpu.VMEM((2, kd // LANES, LANES), f32),
+                pltpu.VMEM((2, kd, LANES), f32),
+                pltpu.VMEM((2, kd // 2, cp), f32),
+                pltpu.VMEM((2, kd // 2, cp), bf16),
+                pltpu.VMEM((2, kd // 2, half), f32),
+                pltpu.VMEM((2, kd // 2, LANES), f32),
                 dma((4,)), dma, dma((nx,)),
                 dma((sweeps, nx)), dma((sweeps, nx)),
                 dma, dma,
-                dma((3, pieces)), dma((3, pieces)), dma((4, pieces)), dma((4, pieces)),
+                dma((2,)), dma((2,)), dma((2,)), dma((2,)),
+                dma((2, nh)), dma((2, nh)), dma((5 + 2 * nh,)), dma((5 + 2 * nh,)),
             ],
             compiler_params=pltpu.CompilerParams(collective_id=0, has_side_effects=True,
                                                  vmem_limit_bytes=48 * 1024 * 1024),

time: 65.9 us -> 61.2 us (0.929)
  Pallas kernels: 65.1 us -> 60.3 us
    pallas_call x1, Pallas kernels: 62.5 us -> 57.7 us  [local_fit(): pl.pallas_call(functools.partial(em_kernel, dims), out_shape=(pltpu.VMEM(...]
where the time goes in v3:
time: 61.2 us; the launch traced here: 61.1 us
  Pallas kernels  60.3 us (99%)
  between operations  0.8 us (1%)
    pallas_call x1, Pallas kernels, local_fit(): pl.pallas_call(functools.partial(em_kernel, dims), out_shape=(pltpu.VMEM(...  57.7 us
    pallas_call x1, Pallas kernels, local_fit(): pl.pallas_call(functools.partial(finish_kernel, fits), out_shape=(jax.Sha...  2.64 us

profile of v3, /device:TPU:97, one launch (start us, length us, event | category | flops | bytes accessed | tf_op | source)
XLA Modules:
  0.0 61.1 jit_solution(10081617998780031624)
XLA Ops:
  0.6 57.7 %shard_map.67 = (f32[2,4096,128]{2,1,0:T(8,128)S(1)}, f32[8,2,8,128]{3,2,1,0:T(8,128)S(1)}) custom-call(f32[3]{0:T(128)} %beta_hbm.1, bf16[256,256]{1,0:T(8,128)(2,1)} %x_hbm.1, f32[2,4096,128]{2,1,0:T(8,128)} %mu_hbm.1, f32[2,4096]{1,0:T(2,128)} %logpi_hbm.1), custom_call_target="tpu_custom_call" | custom-call | tf_op jit(solution)/shard_map/pallas_call | solution.py:464
  58.3 2.6 %shard_map.68 = (f32[2,4096,128]{2,1,0:T(8,128)}, f32[2,4096]{1,0:T(2,128)}, f32[2,256]{1,0:T(2,128)}) custom-call(f32[2,4096,128]{2,1,0:T(8,128)S(1)} %get-tuple-element.5.mu_all, f32[8,2,8,128]{3,2,1,0:T(8,128)S(1)} %get-tuple-element.6.small), custom_call_target="tpu_custom_call" | custom-call | tf_op jit(solution)/shard_map/pallas_call | solution.py:502

commit v4 on v3

--- a/solution.py
+++ b/solution.py
@@ -19,7 +19,7 @@
 
 def em_kernel(dims, beta_hbm, x_hbm, mu_hbm, logpi_hbm, mu_all, small_buf,
               beta_ref, x_ref, logpi_ref, xg, mu_f, mu_b, a_bc, lbuf, rb, s_acc, n_acc,
-              stat_src, stat_buf, small_src, a_row, xm_b, xa_row, xa_bc, xbuf, xrb, xs_acc, xn_acc,
+              stat_src, stat_buf, small_src, a_row, xm_b, xa_row, xa_bc, xbuf_a, xbuf_b, xrb, xs_acc, xn_acc,
               loc_sem, x_send, x_recv, st_send, st_recv, sm_send, sm_recv,
               bk_send, bk_recv, ar_send, ar_recv, far_send, far_recv, sib_send, sib_recv):
     fits, n_comp, n_row, sweeps = dims["fits"], dims["comp"], dims["row"], dims["sweeps"]
@@ -42,15 +42,21 @@
     def dev(c, r):
         return (grp, c, r)
 
+    def hops(k):
+        d_c, d_x = k // nx, k % nx
+        return min(d_c, n_comp - d_c) + min(d_x, nx - d_x)
+
+    peer_order = sorted(range(1, n_peer), key=lambda k: -hops(k))
+    comp_at = [lax.rem(comp + d, n_comp) for d in range(n_comp)]
+    row_at = [lax.rem(xi + d, nx) * fits + fit for d in range(nx)]
+
     def stat_peer(k):
-        d_c, d_x = k // nx, k % nx
-        return lax.rem(comp + d_c, n_comp), lax.rem(xi + d_x, nx)
+        return dev(comp_at[k // nx], row_at[k % nx])
 
     barrier = pltpu.get_barrier_semaphore()
     n_sig = 0
-    for k in range(1, n_peer):
-        c, x = stat_peer(k)
-        pl.semaphore_signal(barrier, inc=1, device_id=dev(c, x * fits + fit), device_id_type=MESH)
+    for k in peer_order:
+        pl.semaphore_signal(barrier, inc=1, device_id=stat_peer(k), device_id_type=MESH)
         n_sig += 1
     for k in range(nx):
         for f in range(1, fits):
@@ -138,14 +144,13 @@
                 ref[1, j:j + 1, :] = r[:, cols]
 
     def stat_copy(t, q, k):
-        c, x = stat_peer(k)
         return pltpu.make_async_remote_copy(
             src_ref=stat_src.at[t, q], dst_ref=stat_buf.at[t, q, me],
             send_sem=st_send.at[t, q], recv_sem=st_recv.at[t, q],
-            device_id=dev(c, x * fits + fit), device_id_type=MESH)
+            device_id=stat_peer(k), device_id_type=MESH)
 
     def stat_start(t, q):
-        for k in range(1, n_peer):
+        for k in peer_order:
             stat_copy(t, q, k).start()
 
     def stat_wait(t, q, send):
@@ -205,13 +210,15 @@
     far = lax.rem(xi + 2, nx)
     sides = ((0, right), (1, left))
 
-    def bulk_piece(p, width):
-        for d, x in sides:
-            rows = pl.ds(p * KB, width * KB)
-            pltpu.make_async_remote_copy(
-                src_ref=mu_b.at[rows], dst_ref=xm_b.at[d, rows],
-                send_sem=bk_send.at[d], recv_sem=bk_recv.at[d],
-                device_id=dev(comp, x * fits + fit), device_id_type=MESH).start()
+    kh = kd // 2
+    nh = kh // KB
+
+    def bulk_copy(d, x, h):
+        rows = slice(h * kh, (h + 1) * kh)
+        return pltpu.make_async_remote_copy(
+            src_ref=mu_b.at[rows], dst_ref=xm_b.at[d, rows],
+            send_sem=bk_send.at[d, h], recv_sem=bk_recv.at[d, h],
+            device_id=dev(comp, x * fits + fit), device_id_type=MESH)
 
     def a_copy(d, x):
         return pltpu.make_async_remote_copy(
@@ -232,11 +239,13 @@
                 mu = s_acc[rows, :] / (cnt + EPS_COUNT)
                 logw = jnp.log((cnt + PRIOR_ALPHA) / (total_pts + total_comp * PRIOR_ALPHA))
                 comp_terms(t + 1, rows, mu, logw)
-                if last:
-                    a_row[b:b + 1, :] = jnp.transpose(a_bc[rows, :])[0:1, :]
+        if last:
+            for d, x in sides:
+                bulk_copy(d, x, d).start()
         e_dot(0)
         if last:
-            bulk_piece(0, 2)
+            for b in range(nkb):
+                a_row[b:b + 1, :] = jnp.transpose(a_bc[b * KB:(b + 1) * KB, :])[0:1, :]
             for d, x in sides:
                 a_copy(d, x).start()
 
@@ -246,8 +255,6 @@
                 e_soft(t + 1, q)
             with jax.named_scope("stsend"):
                 stat_start(t + 1, q)
-                if last:
-                    bulk_piece(q + 2, 1)
             return c
 
         lax.fori_loop(0, nx - 1, e_body, 0)
@@ -255,8 +262,6 @@
             e_soft(t + 1, nx - 1)
         with jax.named_scope("stsend"):
             stat_start(t + 1, nx - 1)
-            if last:
-                bulk_piece(nx + 1, nkb - nx - 1)
 
     def sweep_body(t, c):
         sweep(t, False)
@@ -273,43 +278,59 @@
         sq_rows.append(jnp.sum(jnp.transpose(xb * xb), axis=0, keepdims=True))
     sq = jnp.concatenate(sq_rows, axis=0)
 
-    kh = kd // 2
-    nh = kh // KB
     c2_last = beta_ref[tl] * (2.0 * LOG2E)
     sib = xi * fits + lax.rem(fit + 1, fits)
-    with jax.named_scope("bulkwait"):
+
+    for d, x in sides:
+        bulk_copy(d, x, 1 - d).start()
+
+    def x_ready(halves):
+        with jax.named_scope("bulkwait"):
+            for d, h in enumerate(halves):
+                bulk_copy(d, left, h).wait_recv()
+
+    def x_terms(halves):
+        with jax.named_scope("xterms"):
+            for d, h in enumerate(halves):
+                for b in range(h * nh, (h + 1) * nh):
+                    xa_bc[d, b * KB:(b + 1) * KB, :] = jnp.transpose(jnp.broadcast_to(xa_row[d, b:b + 1, :], (KB, LANES)))
+
+    x_ready((0, 1))
+    owner = (comp * nx + left, comp * nx + right)
+
+    def x_dot(buf, q, halves):
+        for d, h in enumerate(halves):
+            buf[d] = lax.dot_general(xm_b[d, h * kh:(h + 1) * kh, :], xg[q], NT, preferred_element_type=jnp.float32)
+
+    def x_scales(q):
+        m, r = totals_of(tl, q)
+        res = []
         for d in range(2):
-            pltpu.make_async_copy(xm_b.at[d], xm_b.at[d], bk_recv.at[d]).wait()
-            pltpu.make_async_copy(xa_row.at[d], xa_row.at[d], ar_recv.at[d]).wait()
-    with jax.named_scope("xterms"):
-        for d in range(2):
-            for b in range(nkb):
-                xa_bc[d, b * KB:(b + 1) * KB, :] = jnp.transpose(jnp.broadcast_to(xa_row[d, b:b + 1, :], (KB, LANES)))
-
-    owner = (comp * nx + left, comp * nx + right)
-
-    def x_units(q, first, halves):
-        m, r = totals_of(tl, q)
+            m_j = stat_buf[tl, q, owner[d], 0]
+            res.append((lane_rows(m_j, KB), lane_rows(jnp.exp2(m_j - m) / r, KB)))
+        return res
+
+    def x_resp(buf, q, d, h, scales, first):
+        m_row, sc_row = scales[d]
+        for b in range(nh):
+            rows = slice(b * KB, (b + 1) * KB)
+            l = buf[d, rows, :] * c2_last + lanes_tile(xa_bc[d, h * kh + b * KB:h * kh + (b + 1) * KB, :])
+            res = jnp.exp2(l - m_row) * sc_row
+            cnt = res[:, 0:LANES]
+            for j in range(1, lb):
+                cnt = cnt + res[:, j * LANES:(j + 1) * LANES]
+            xrb[q, d, rows, :] = res.astype(jnp.bfloat16)
+            xn_acc[d, rows, :] = jnp.where(first, cnt, xn_acc[d, rows, :] + cnt)
+
+    def x_sum(q, d, first):
+        s = jnp.dot(xrb[q, d], xg[q], preferred_element_type=jnp.float32)
+        xs_acc[d] = jnp.where(first, s, xs_acc[d] + s)
+
+    def x_units(buf, q, first, halves):
+        scales = x_scales(q)
         for d, h in enumerate(halves):
-            hrows = slice(h * kh, (h + 1) * kh)
-            xbuf[d] = lax.dot_general(xm_b[d, hrows, :], xg[q], NT, preferred_element_type=jnp.float32)
-        for d, h in enumerate(halves):
-            m_j = stat_buf[tl, q, owner[d], 0]
-            m_row = lane_rows(m_j, KB)
-            sc_row = lane_rows(jnp.exp2(m_j - m) / r, KB)
-            for b in range(nh):
-                rows = slice(b * KB, (b + 1) * KB)
-                grows = slice(h * kh + b * KB, h * kh + (b + 1) * KB)
-                l = xbuf[d, rows, :] * c2_last + lanes_tile(xa_bc[d, grows, :])
-                res = jnp.exp2(l - m_row) * sc_row
-                cnt = res[:, 0:LANES]
-                for j in range(1, lb):
-                    cnt = cnt + res[:, j * LANES:(j + 1) * LANES]
-                xrb[d, rows, :] = res.astype(jnp.bfloat16)
-                xn_acc[d, rows, :] = jnp.where(first, cnt, xn_acc[d, rows, :] + cnt)
-        for d, h in enumerate(halves):
-            s = jnp.dot(xrb[d], xg[q], preferred_element_type=jnp.float32)
-            xs_acc[d] = jnp.where(first, s, xs_acc[d] + s)
+            x_resp(buf, q, d, h, scales, first)
+            x_sum(q, d, first)
 
     def mean_rows(na, sa):
         return sa / (jnp.sum(na, axis=1, keepdims=True) + EPS_COUNT)
@@ -331,26 +352,49 @@
         rows = slice(b * KB, (b + 1) * KB)
         mu_all[fit, span(x, h * kh + b * KB, KB), :] = mean_rows(xn_acc[d, rows, :], xs_acc[d, rows, :])
 
+    with jax.named_scope("xdotA"):
+        for q in range(nx):
+            x_dot(xbuf_a.at[q], q, (0, 1))
+    with jax.named_scope("arwait"):
+        for d in range(2):
+            a_copy(d, left).wait_recv()
+    x_terms((0, 1))
+    x_terms((1, 0))
+
+    def x_last(buf, q, halves, done):
+        scales = x_scales(q)
+        for d, h in enumerate(halves):
+            x_resp(buf, q, d, h, scales, False)
+            x_sum(q, d, False)
+            for b in range(nh):
+                x_finish(d, h, b)
+            for b in range(nh):
+                done(d, h, b)
+
     def xa_body(q, c):
         stat_wait(tl, q, False)
         with jax.named_scope("xunitA"):
-            x_units(q, q == 0, (0, 1))
-        return c
-
-    lax.fori_loop(0, nx, xa_body, 0)
-    with jax.named_scope("xfinA"):
-        for b in range(nh):
-            for d, x in sides:
-                x_finish(d, d, b)
-                push((left, right)[d], d * kh + b * KB, KB, far_send.at[d, b], far_recv.at[d, b], x * fits + fit)
-        for d in range(2):
-            push((left, right)[d], d * kh, kh, sib_send.at[d], sib_recv.at[d], sib)
-
-    def m_last(q, c):
+            x_units(xbuf_a.at[q], q, q == 0, (0, 1))
         m_chunk(tl, q, q == 0)
         return c
 
-    lax.fori_loop(0, nx, m_last, 0)
+    lax.fori_loop(0, nx - 2, xa_body, 0)
+    stat_wait(tl, nx - 2, False)
+    with jax.named_scope("xunitA"):
+        x_units(xbuf_a.at[nx - 2], nx - 2, False, (0, 1))
+    ql = nx - 1
+    stat_wait(tl, ql, False)
+
+    def a_done(d, h, b):
+        x = (left, right)[d]
+        push(x, h * kh + b * KB, KB, far_send.at[d, b], far_recv.at[d, b], sides[d][1] * fits + fit)
+        if b == nh - 1:
+            push(x, h * kh, kh, sib_send.at[d], sib_recv.at[d], sib)
+
+    with jax.named_scope("xfinA"):
+        x_last(xbuf_a.at[ql], ql, (0, 1), a_done)
+    m_chunk(tl, nx - 2, False)
+    m_chunk(tl, ql, False)
     with jax.named_scope("ownfin"):
         m, r, _ = scale_of(tl, xi)
         small_src[1, 0:lb, :] = m * LN2 + jnp.log(r) - beta_ref[tl] * sq
@@ -368,24 +412,34 @@
             cpy.start()
         small_buf[row] = small_src[...]
 
-    def xb_body(q, c):
-        with jax.named_scope("xunitB"):
-            x_units(q, q == 0, (1, 0))
-        return c
-
-    lax.fori_loop(0, nx, xb_body, 0)
+    x_ready((1, 0))
+    with jax.named_scope("xunitB"):
+        x_dot(xbuf_b.at[0], 0, (1, 0))
+        for q in range(nx - 1):
+            x_dot(xbuf_b.at[q + 1], q + 1, (1, 0))
+            scales = x_scales(q)
+            for d, h in enumerate((1, 0)):
+                x_resp(xbuf_b.at[q], q, d, h, scales, q == 0)
+            if q > 0:
+                for d in range(2):
+                    x_sum(q - 1, d, q == 1)
+        for d in range(2):
+            x_sum(nx - 2, d, False)
+
+    def b_done(d, h, b):
+        if b % 2:
+            k = 3 + 2 * d + b // 2
+            push((left, right)[d], h * kh + (b - 1) * KB, 2 * KB, sib_send.at[k], sib_recv.at[k], sib)
+
     with jax.named_scope("xfinB"):
-        for d in range(2):
-            for b in range(nh):
-                x_finish(d, 1 - d, b)
-            push((left, right)[d], (1 - d) * kh, kh, sib_send.at[3 + d], sib_recv.at[3 + d], sib)
+        x_last(xbuf_b.at[ql], ql, (1, 0), b_done)
 
     with jax.named_scope("farwait"):
         for b in range(nh):
             for d in range(2):
                 part = mu_all.at[fit, span(far, d * kh + b * KB, KB)]
                 pltpu.make_async_copy(part, part, far_recv.at[d, b]).wait()
-                k = 5 + d * nh + b
+                k = 7 + d * nh + b
                 push(far, d * kh + b * KB, KB, sib_send.at[k], sib_recv.at[k], sib)
     ofit = lax.rem(fit + 1, fits)
 
@@ -397,9 +451,10 @@
         sib_wait(xi, 0, kd, 2)
         for d, x in ((0, left), (1, right)):
             sib_wait(x, d * kh, kh, d)
-            sib_wait(x, (1 - d) * kh, kh, 3 + d)
+            sib_wait(x, (1 - d) * kh, kh // 2, 3 + 2 * d)
+            sib_wait(x, (1 - d) * kh + kh // 2, kh // 2, 4 + 2 * d)
             for b in range(nh):
-                sib_wait(far, d * kh + b * KB, KB, 5 + d * nh + b)
+                sib_wait(far, d * kh + b * KB, KB, 7 + d * nh + b)
 
     part = small_buf.at[pl.ds(0, n_row - 1)]
     pltpu.make_async_copy(part, part, sm_recv).wait()
@@ -414,13 +469,17 @@
     for cpy in x_copies:
         cpy.wait_send()
     for d in range(2):
-        pltpu.make_async_copy(xm_b.at[d], xm_b.at[d], bk_send.at[d]).wait()
-        pltpu.make_async_copy(xa_row.at[d], xa_row.at[d], ar_send.at[d]).wait()
+        bulk_copy(d, left, 0).wait_send()
+        bulk_copy(d, left, 1).wait_send()
+        a_copy(d, left).wait_send()
 
 
 def finish_kernel(fits, mu_all, small, o_mu, o_logpi, o_lse, sem):
-    cp = pltpu.make_async_copy(mu_all, o_mu, sem)
-    cp.start()
+    step = mu_all.shape[1] // 8
+    for f in range(fits):
+        for p in range(8):
+            part = pl.ds(p * step, step)
+            pltpu.make_async_copy(mu_all.at[f, part], o_mu.at[f, part], sem).start()
     row = lax.axis_index("row")
     fit = lax.rem(row, fits)
     first = row - fit
@@ -438,7 +497,7 @@
             for g in range(1, fits):
                 v = jnp.where(fit == g, small[first + f, 1, g * per + j:g * per + j + 1, :], v)
             o_lse[f:f + 1, j * LANES:(j + 1) * LANES] = v
-    cp.wait()
+    pltpu.make_async_copy(mu_all, o_mu, sem).wait()
 
 
 def solution(mesh):
@@ -486,15 +545,16 @@
                 pltpu.VMEM((2, kd, half), bf16),
                 pltpu.VMEM((2, kd // LANES, LANES), f32),
                 pltpu.VMEM((2, kd, LANES), f32),
-                pltpu.VMEM((2, kd // 2, cp), f32),
-                pltpu.VMEM((2, kd // 2, cp), bf16),
+                pltpu.VMEM((nx, 2, kd // 2, cp), f32),
+                pltpu.VMEM((nx, 2, kd // 2, cp), f32),
+                pltpu.VMEM((nx, 2, kd // 2, cp), bf16),
                 pltpu.VMEM((2, kd // 2, half), f32),
                 pltpu.VMEM((2, kd // 2, LANES), f32),
                 dma((4,)), dma, dma((nx,)),
                 dma((sweeps, nx)), dma((sweeps, nx)),
                 dma, dma,
-                dma((2,)), dma((2,)), dma((2,)), dma((2,)),
-                dma((2, nh)), dma((2, nh)), dma((5 + 2 * nh,)), dma((5 + 2 * nh,)),
+                dma((2, 2)), dma((2, 2)), dma((2,)), dma((2,)),
+                dma((2, nh)), dma((2, nh)), dma((7 + 2 * nh,)), dma((7 + 2 * nh,)),
             ],
             compiler_params=pltpu.CompilerParams(collective_id=0, has_side_effects=True,
                                                  vmem_limit_bytes=48 * 1024 * 1024),

time: 61.2 us -> 56.4 us (0.922)
  Pallas kernels: 60.3 us -> 55.5 us
    pallas_call x1, Pallas kernels: 57.7 us -> 52.9 us  [local_fit(): pl.pallas_call(functools.partial(em_kernel, dims), out_shape=(pltpu.VMEM(...]
where the time goes in v4:
time: 56.4 us; the launch traced here: 56.3 us
  Pallas kernels  55.5 us (98%)
  between operations  0.82 us (1%)
    pallas_call x1, Pallas kernels, local_fit(): pl.pallas_call(functools.partial(em_kernel, dims), out_shape=(pltpu.VMEM(...  52.9 us
    pallas_call x1, Pallas kernels, local_fit(): pl.pallas_call(functools.partial(finish_kernel, fits), out_shape=(jax.Sha...  2.62 us

profile of v4, /device:TPU:97, one launch (start us, length us, event | category | flops | bytes accessed | tf_op | source)
XLA Modules:
  0.0 56.3 jit_solution(3482390474333385112)
XLA Ops:
  0.6 52.9 %shard_map.67 = (f32[2,4096,128]{2,1,0:T(8,128)S(1)}, f32[8,2,8,128]{3,2,1,0:T(8,128)S(1)}) custom-call(f32[3]{0:T(128)} %beta_hbm.1, bf16[256,256]{1,0:T(8,128)(2,1)} %x_hbm.1, f32[2,4096,128]{2,1,0:T(8,128)} %mu_hbm.1, f32[2,4096]{1,0:T(2,128)} %logpi_hbm.1), custom_call_target="tpu_custom_call" | custom-call | tf_op jit(solution)/shard_map/pallas_call | solution.py:523
  53.5 2.6 %shard_map.68 = (f32[2,4096,128]{2,1,0:T(8,128)}, f32[2,4096]{1,0:T(2,128)}, f32[2,256]{1,0:T(2,128)}) custom-call(f32[2,4096,128]{2,1,0:T(8,128)S(1)} %get-tuple-element.5.mu_all, f32[8,2,8,128]{3,2,1,0:T(8,128)S(1)} %get-tuple-element.6.small), custom_call_target="tpu_custom_call" | custom-call | tf_op jit(solution)/shard_map/pallas_call | solution.py:562

commit v5 on v4

--- a/solution.py
+++ b/solution.py
@@ -19,7 +19,7 @@
 
 def em_kernel(dims, beta_hbm, x_hbm, mu_hbm, logpi_hbm, mu_all, small_buf,
               beta_ref, x_ref, logpi_ref, xg, mu_f, mu_b, a_bc, lbuf, rb, s_acc, n_acc,
-              stat_src, stat_buf, small_src, a_row, xm_b, xa_row, xa_bc, xbuf_a, xbuf_b, xrb, xs_acc, xn_acc,
+              stat_src, stat_buf, mx, small_src, a_row, xm_b, xa_row, xa_bc, xbuf_a, xbuf_b, xrb, xs_acc, xn_acc,
               loc_sem, x_send, x_recv, st_send, st_recv, sm_send, sm_recv,
               bk_send, bk_recv, ar_send, ar_recv, far_send, far_recv, sib_send, sib_recv):
     fits, n_comp, n_row, sweeps = dims["fits"], dims["comp"], dims["row"], dims["sweeps"]
@@ -78,16 +78,7 @@
         a_bc[rows, :] = jnp.broadcast_to(a, (a.shape[0], LANES))
         mu_b[rows, :] = mu.astype(jnp.bfloat16)
 
-    for cpy in loads:
-        cpy.wait()
-    for b in range(kd // LANES):
-        rows = pl.ds(b * LANES, LANES)
-        lw = logpi_ref[:, pl.ds(pl.multiple_of(xi * kd + b * LANES, LANES), LANES)]
-        pick = lax.broadcasted_iota(jnp.int32, (fits, LANES), 0) == fit
-        lw = jnp.sum(jnp.where(pick, lw, 0.0), axis=0, keepdims=True)
-        lw = jnp.transpose(jnp.broadcast_to(lw, (LANES, LANES)))
-        comp_terms(0, rows, mu_f[rows, :], lw[:, 0:1])
-
+    loads[0].wait()
     with jax.named_scope("bar"):
         pl.semaphore_wait(barrier, n_sig)
 
@@ -111,25 +102,39 @@
             x_copies.append(cpy)
     xg[xi, my_rows, :] = x_ref[:, x_cols(fit)]
 
+    for cpy in loads[1:]:
+        cpy.wait()
+    for b in range(kd // LANES):
+        rows = pl.ds(b * LANES, LANES)
+        lw = logpi_ref[:, pl.ds(pl.multiple_of(xi * kd + b * LANES, LANES), LANES)]
+        pick = lax.broadcasted_iota(jnp.int32, (fits, LANES), 0) == fit
+        lw = jnp.sum(jnp.where(pick, lw, 0.0), axis=0, keepdims=True)
+        lw = jnp.transpose(jnp.broadcast_to(lw, (LANES, LANES)))
+        comp_terms(0, rows, mu_f[rows, :], lw[:, 0:1])
+    for ref in (n_acc, s_acc, xn_acc, xs_acc):
+        ref[...] = jnp.zeros(ref.shape, jnp.float32)
+
     def lanes_tile(v):
         return jnp.concatenate([v] * lb, axis=1)
 
     KB = 128
     nkb = kd // KB
 
-    def e_dot(q):
+    def e_dot(t, q):
+        c2 = beta_ref[t] * (2.0 * LOG2E)
         with jax.named_scope("edot"):
-            lbuf[q] = lax.dot_general(mu_b[...], xg[q], NT, preferred_element_type=jnp.float32)
+            a = lax.dot_general(mu_b[...], xg[q], NT, preferred_element_type=jnp.float32)
+            m8 = None
+            for b in range(nkb):
+                rows = slice(b * KB, (b + 1) * KB)
+                l = a[rows, :] * c2 + lanes_tile(a_bc[rows, :])
+                lbuf[q, rows, :] = l
+                mb = jnp.max(l.reshape(KB // 8, 8, cp), axis=0)
+                m8 = mb if m8 is None else jnp.maximum(m8, mb)
+            mx[q] = m8
 
     def e_soft(t, q):
-        c2 = beta_ref[t] * (2.0 * LOG2E)
-        m8 = jnp.full((8, cp), -jnp.inf, jnp.float32)
-        for b in range(nkb):
-            rows = slice(b * KB, (b + 1) * KB)
-            l = lbuf[q, rows, :] * c2 + lanes_tile(a_bc[rows, :])
-            lbuf[q, rows, :] = l
-            m8 = jnp.maximum(m8, jnp.max(l.reshape(KB // 8, 8, cp), axis=0))
-        m = jnp.max(m8, axis=0, keepdims=True)
+        m = jnp.max(mx[q], axis=0, keepdims=True)
         r8 = jnp.zeros((8, cp), jnp.float32)
         for b in range(nkb):
             rows = slice(b * KB, (b + 1) * KB)
@@ -182,15 +187,14 @@
         rb[rows, :] = res.astype(jnp.bfloat16)
         return cnt
 
-    def m_chunk(t, q, first):
+    def m_chunk(t, q):
         m, r, sc = scale_of(t, q)
         with jax.named_scope("mchunk"):
             for b in range(nkb):
                 rows = slice(b * KB, (b + 1) * KB)
                 cnt = m_rows(q, rows, KB, sc)
-                n_acc[rows, :] = jnp.where(first, cnt, n_acc[rows, :] + cnt)
-            s = jnp.dot(rb[...], xg[q], preferred_element_type=jnp.float32)
-            s_acc[...] = jnp.where(first, s, s_acc[...] + s)
+                n_acc[rows, :] += cnt
+            s_acc[...] += jnp.dot(rb[...], xg[q], preferred_element_type=jnp.float32)
         return m, r
 
     order = (0, 1, 3, 2) if nx == 4 else tuple(range(nx))
@@ -200,7 +204,7 @@
         part = xg.at[q, pl.ds(0, n_in * n_rows)]
         with jax.named_scope("xwait"):
             pltpu.make_async_copy(part, part, x_recv.at[q]).wait()
-        e_dot(q)
+        e_dot(0, q)
         with jax.named_scope("esoft"):
             e_soft(0, q)
         stat_start(0, q)
@@ -228,7 +232,7 @@
     def sweep(t, last):
         def m_body(q, c):
             stat_wait(t, q, False)
-            m_chunk(t, q, q == 0)
+            m_chunk(t, q)
             return c
 
         lax.fori_loop(0, nx, m_body, 0)
@@ -239,10 +243,12 @@
                 mu = s_acc[rows, :] / (cnt + EPS_COUNT)
                 logw = jnp.log((cnt + PRIOR_ALPHA) / (total_pts + total_comp * PRIOR_ALPHA))
                 comp_terms(t + 1, rows, mu, logw)
+                n_acc[rows, :] = jnp.zeros((KB, LANES), jnp.float32)
+                s_acc[rows, :] = jnp.zeros((KB, half), jnp.float32)
         if last:
             for d, x in sides:
                 bulk_copy(d, x, d).start()
-        e_dot(0)
+        e_dot(t + 1, 0)
         if last:
             for b in range(nkb):
                 a_row[b:b + 1, :] = jnp.transpose(a_bc[b * KB:(b + 1) * KB, :])[0:1, :]
@@ -250,7 +256,7 @@
                 a_copy(d, x).start()
 
         def e_body(q, c):
-            e_dot(q + 1)
+            e_dot(t + 1, q + 1)
             with jax.named_scope("esoft"):
                 e_soft(t + 1, q)
             with jax.named_scope("stsend"):
@@ -300,7 +306,10 @@
 
     def x_dot(buf, q, halves):
         for d, h in enumerate(halves):
-            buf[d] = lax.dot_general(xm_b[d, h * kh:(h + 1) * kh, :], xg[q], NT, preferred_element_type=jnp.float32)
+            a = lax.dot_general(xm_b[d, h * kh:(h + 1) * kh, :], xg[q], NT, preferred_element_type=jnp.float32)
+            for b in range(nh):
+                rows = slice(b * KB, (b + 1) * KB)
+                buf[d, rows, :] = a[rows, :] * c2_last + lanes_tile(xa_bc[d, h * kh + b * KB:h * kh + (b + 1) * KB, :])
 
     def x_scales(q):
         m, r = totals_of(tl, q)
@@ -310,27 +319,25 @@
             res.append((lane_rows(m_j, KB), lane_rows(jnp.exp2(m_j - m) / r, KB)))
         return res
 
-    def x_resp(buf, q, d, h, scales, first):
+    def x_resp(buf, q, s_at, d, h, scales):
         m_row, sc_row = scales[d]
         for b in range(nh):
             rows = slice(b * KB, (b + 1) * KB)
-            l = buf[d, rows, :] * c2_last + lanes_tile(xa_bc[d, h * kh + b * KB:h * kh + (b + 1) * KB, :])
-            res = jnp.exp2(l - m_row) * sc_row
+            res = jnp.exp2(buf[d, rows, :] - m_row) * sc_row
             cnt = res[:, 0:LANES]
             for j in range(1, lb):
                 cnt = cnt + res[:, j * LANES:(j + 1) * LANES]
             xrb[q, d, rows, :] = res.astype(jnp.bfloat16)
-            xn_acc[d, rows, :] = jnp.where(first, cnt, xn_acc[d, rows, :] + cnt)
-
-    def x_sum(q, d, first):
-        s = jnp.dot(xrb[q, d], xg[q], preferred_element_type=jnp.float32)
-        xs_acc[d] = jnp.where(first, s, xs_acc[d] + s)
-
-    def x_units(buf, q, first, halves):
+            xn_acc[s_at, d, rows, :] += cnt
+
+    def x_sum(q, s_at, d):
+        xs_acc[s_at, d] += jnp.dot(xrb[q, d], xg[q], preferred_element_type=jnp.float32)
+
+    def x_units(buf, q, s_at, halves):
         scales = x_scales(q)
         for d, h in enumerate(halves):
-            x_resp(buf, q, d, h, scales, first)
-            x_sum(q, d, first)
+            x_resp(buf, q, s_at, d, h, scales)
+            x_sum(q, s_at, d)
 
     def mean_rows(na, sa):
         return sa / (jnp.sum(na, axis=1, keepdims=True) + EPS_COUNT)
@@ -347,41 +354,41 @@
         cpy.start()
         waits.append(cpy.wait_send)
 
-    def x_finish(d, h, b):
+    def x_finish(s_at, d, h, b):
         x = (left, right)[d]
         rows = slice(b * KB, (b + 1) * KB)
-        mu_all[fit, span(x, h * kh + b * KB, KB), :] = mean_rows(xn_acc[d, rows, :], xs_acc[d, rows, :])
-
-    with jax.named_scope("xdotA"):
-        for q in range(nx):
-            x_dot(xbuf_a.at[q], q, (0, 1))
+        mu_all[fit, span(x, h * kh + b * KB, KB), :] = mean_rows(xn_acc[s_at, d, rows, :], xs_acc[s_at, d, rows, :])
+
     with jax.named_scope("arwait"):
         for d in range(2):
             a_copy(d, left).wait_recv()
     x_terms((0, 1))
     x_terms((1, 0))
-
-    def x_last(buf, q, halves, done):
+    with jax.named_scope("xdotA"):
+        for q in range(nx):
+            x_dot(xbuf_a.at[q], q, (0, 1))
+
+    def x_last(buf, q, s_at, halves, done):
         scales = x_scales(q)
         for d, h in enumerate(halves):
-            x_resp(buf, q, d, h, scales, False)
-            x_sum(q, d, False)
+            x_resp(buf, q, s_at, d, h, scales)
+            x_sum(q, s_at, d)
             for b in range(nh):
-                x_finish(d, h, b)
+                x_finish(s_at, d, h, b)
             for b in range(nh):
                 done(d, h, b)
 
     def xa_body(q, c):
         stat_wait(tl, q, False)
         with jax.named_scope("xunitA"):
-            x_units(xbuf_a.at[q], q, q == 0, (0, 1))
-        m_chunk(tl, q, q == 0)
+            x_units(xbuf_a.at[q], q, 0, (0, 1))
+        m_chunk(tl, q)
         return c
 
     lax.fori_loop(0, nx - 2, xa_body, 0)
     stat_wait(tl, nx - 2, False)
     with jax.named_scope("xunitA"):
-        x_units(xbuf_a.at[nx - 2], nx - 2, False, (0, 1))
+        x_units(xbuf_a.at[nx - 2], nx - 2, 0, (0, 1))
     ql = nx - 1
     stat_wait(tl, ql, False)
 
@@ -392,9 +399,9 @@
             push(x, h * kh, kh, sib_send.at[d], sib_recv.at[d], sib)
 
     with jax.named_scope("xfinA"):
-        x_last(xbuf_a.at[ql], ql, (0, 1), a_done)
-    m_chunk(tl, nx - 2, False)
-    m_chunk(tl, ql, False)
+        x_last(xbuf_a.at[ql], ql, 0, (0, 1), a_done)
+    m_chunk(tl, nx - 2)
+    m_chunk(tl, ql)
     with jax.named_scope("ownfin"):
         m, r, _ = scale_of(tl, xi)
         small_src[1, 0:lb, :] = m * LN2 + jnp.log(r) - beta_ref[tl] * sq
@@ -419,12 +426,12 @@
             x_dot(xbuf_b.at[q + 1], q + 1, (1, 0))
             scales = x_scales(q)
             for d, h in enumerate((1, 0)):
-                x_resp(xbuf_b.at[q], q, d, h, scales, q == 0)
+                x_resp(xbuf_b.at[q], q, 1, d, h, scales)
             if q > 0:
                 for d in range(2):
-                    x_sum(q - 1, d, q == 1)
+                    x_sum(q - 1, 1, d)
         for d in range(2):
-            x_sum(nx - 2, d, False)
+            x_sum(nx - 2, 1, d)
 
     def b_done(d, h, b):
         if b % 2:
@@ -432,7 +439,7 @@
             push((left, right)[d], h * kh + (b - 1) * KB, 2 * KB, sib_send.at[k], sib_recv.at[k], sib)
 
     with jax.named_scope("xfinB"):
-        x_last(xbuf_b.at[ql], ql, (1, 0), b_done)
+        x_last(xbuf_b.at[ql], ql, 1, (1, 0), b_done)
 
     with jax.named_scope("farwait"):
         for b in range(nh):
@@ -474,30 +481,37 @@
         a_copy(d, left).wait_send()
 
 
-def finish_kernel(fits, mu_all, small, o_mu, o_logpi, o_lse, sem):
-    step = mu_all.shape[1] // 8
-    for f in range(fits):
-        for p in range(8):
-            part = pl.ds(p * step, step)
-            pltpu.make_async_copy(mu_all.at[f, part], o_mu.at[f, part], sem).start()
+def finish_kernel(fits, mu_all, small, o_mu, o_logpi, o_lse, logpi_buf, lse_buf, sems):
     row = lax.axis_index("row")
     fit = lax.rem(row, fits)
     first = row - fit
-    n_row, _, srows, _ = small.shape
+    n_row = small.shape[0]
     nx = n_row // fits
     kd = o_logpi.shape[1] // nx
-    n_rows = o_lse.shape[1]
-    per = n_rows // LANES
+    per = o_lse.shape[1] // LANES
+    parts = 4
+    step = mu_all.shape[1] // parts
+    copies = []
     for f in range(fits):
-        for x in range(nx):
-            for j in range(kd // LANES):
-                o_logpi[f:f + 1, x * kd + j * LANES:x * kd + (j + 1) * LANES] = small[x * fits + f, 0, j:j + 1, :]
+        for p in range(parts):
+            part = pl.ds(p * step, step)
+            copies.append(pltpu.make_async_copy(mu_all.at[f, part], o_mu.at[f, part], sems.at[f * parts + p]))
+            copies[-1].start()
+    for f in range(fits):
         for j in range(per):
             v = small[first + f, 1, j:j + 1, :]
             for g in range(1, fits):
                 v = jnp.where(fit == g, small[first + f, 1, g * per + j:g * per + j + 1, :], v)
-            o_lse[f:f + 1, j * LANES:(j + 1) * LANES] = v
-    pltpu.make_async_copy(mu_all, o_mu, sem).wait()
+            lse_buf[f:f + 1, j * LANES:(j + 1) * LANES] = v
+        for x in range(nx):
+            for j in range(kd // LANES):
+                logpi_buf[f:f + 1, x * kd + j * LANES:x * kd + (j + 1) * LANES] = small[x * fits + f, 0, j:j + 1, :]
+    n = fits * parts
+    for k, (src, dst) in enumerate(((logpi_buf, o_logpi), (lse_buf, o_lse))):
+        copies.append(pltpu.make_async_copy(src, dst, sems.at[n + k]))
+        copies[-1].start()
+    for c in copies:
+        c.wait()
 
 
 def solution(mesh):
@@ -540,6 +554,7 @@
                 pltpu.VMEM((kd, LANES), f32),
                 pltpu.VMEM((sweeps, nx, 2, srows, LANES), f32),
                 pltpu.VMEM((sweeps, nx, n_peer, 2, srows, LANES), f32),
+                pltpu.VMEM((nx, 8, cp), f32),
                 pltpu.VMEM((2, kd // LANES, LANES), f32),
                 pltpu.VMEM((kd // LANES, LANES), f32),
                 pltpu.VMEM((2, kd, half), bf16),
@@ -548,8 +563,8 @@
                 pltpu.VMEM((nx, 2, kd // 2, cp), f32),
                 pltpu.VMEM((nx, 2, kd // 2, cp), f32),
                 pltpu.VMEM((nx, 2, kd // 2, cp), bf16),
-                pltpu.VMEM((2, kd // 2, half), f32),
-                pltpu.VMEM((2, kd // 2, LANES), f32),
+                pltpu.VMEM((2, 2, kd // 2, half), f32),
+                pltpu.VMEM((2, 2, kd // 2, LANES), f32),
                 dma((4,)), dma, dma((nx,)),
                 dma((sweeps, nx)), dma((sweeps, nx)),
                 dma, dma,
@@ -565,8 +580,8 @@
                        jax.ShapeDtypeStruct((fits, n_local), f32),
                        jax.ShapeDtypeStruct((fits, n_rows), f32)),
             in_specs=[pl.BlockSpec(memory_space=pl.ANY), vmem],
-            out_specs=(hbm, vmem, vmem),
-            scratch_shapes=[dma],
+            out_specs=(hbm, hbm, hbm),
+            scratch_shapes=[pltpu.VMEM((fits, n_local), f32), pltpu.VMEM((fits, n_rows), f32), dma((4 * fits + 2,))],
             compiler_params=pltpu.CompilerParams(vmem_limit_bytes=8 * 1024 * 1024),
         )(pltpu.with_memory_space_constraint(mu, pltpu.VMEM), pltpu.with_memory_space_constraint(small, pltpu.VMEM))
 

time: 56.4 us -> 55.3 us (0.980)
  Pallas kernels: 55.5 us -> 54.4 us
    pallas_call x1, Pallas kernels: 52.9 us -> 52.3 us  [local_fit(): pl.pallas_call(functools.partial(em_kernel, dims), out_shape=(pltpu.VMEM(...]
where the time goes in v5:
time: 55.3 us; the launch traced here: 55.2 us
  Pallas kernels  54.4 us (98%)
  between operations  0.8 us (1%)
    pallas_call x1, Pallas kernels, local_fit(): pl.pallas_call(functools.partial(em_kernel, dims), out_shape=(pltpu.VMEM(...  52.3 us
    pallas_call x1, Pallas kernels, local_fit(): pl.pallas_call(functools.partial(finish_kernel, fits), out_shape=(jax.Sha...  2.09 us

profile of v5, /device:TPU:97, one launch (start us, length us, event | category | flops | bytes accessed | tf_op | source)
XLA Modules:
  0.0 55.2 jit_solution(4006709986207823920)
XLA Ops:
  0.6 52.3 %shard_map.67 = (f32[2,4096,128]{2,1,0:T(8,128)S(1)}, f32[8,2,8,128]{3,2,1,0:T(8,128)S(1)}) custom-call(f32[3]{0:T(128)} %beta_hbm.1, bf16[256,256]{1,0:T(8,128)(2,1)} %x_hbm.1, f32[2,4096,128]{2,1,0:T(8,128)} %mu_hbm.1, f32[2,4096]{1,0:T(2,128)} %logpi_hbm.1), custom_call_target="tpu_custom_call" | custom-call | tf_op jit(solution)/shard_map/pallas_call | solution.py:537
  52.9 2.1 %shard_map.68 = (f32[2,4096,128]{2,1,0:T(8,128)}, f32[2,4096]{1,0:T(2,128)}, f32[2,256]{1,0:T(2,128)}) custom-call(f32[2,4096,128]{2,1,0:T(8,128)S(1)} %get-tuple-element.5.mu_all, f32[8,2,8,128]{3,2,1,0:T(8,128)S(1)} %get-tuple-element.6.small), custom_call_target="tpu_custom_call" | custom-call | tf_op jit(solution)/shard_map/pallas_call | solution.py:577

commit v6 on v5

--- a/solution.py
+++ b/solution.py
@@ -256,11 +256,11 @@
                 a_copy(d, x).start()
 
         def e_body(q, c):
-            e_dot(t + 1, q + 1)
             with jax.named_scope("esoft"):
                 e_soft(t + 1, q)
             with jax.named_scope("stsend"):
                 stat_start(t + 1, q)
+            e_dot(t + 1, q + 1)
             return c
 
         lax.fori_loop(0, nx - 1, e_body, 0)
@@ -382,7 +382,6 @@
         stat_wait(tl, q, False)
         with jax.named_scope("xunitA"):
             x_units(xbuf_a.at[q], q, 0, (0, 1))
-        m_chunk(tl, q)
         return c
 
     lax.fori_loop(0, nx - 2, xa_body, 0)
@@ -400,8 +399,12 @@
 
     with jax.named_scope("xfinA"):
         x_last(xbuf_a.at[ql], ql, 0, (0, 1), a_done)
-    m_chunk(tl, nx - 2)
-    m_chunk(tl, ql)
+
+    def own_body(q, c):
+        m_chunk(tl, q)
+        return c
+
+    lax.fori_loop(0, nx, own_body, 0)
     with jax.named_scope("ownfin"):
         m, r, _ = scale_of(tl, xi)
         small_src[1, 0:lb, :] = m * LN2 + jnp.log(r) - beta_ref[tl] * sq

time: 55.3 us -> 55.2 us (level)
  no operation moved by 1% of the time
where the time goes in v6:
time: 55.2 us; the launch traced here: 55.1 us
  Pallas kernels  54.3 us (98%)
  between operations  0.82 us (1%)
    pallas_call x1, Pallas kernels, local_fit(): pl.pallas_call(functools.partial(em_kernel, dims), out_shape=(pltpu.VMEM(...  52.2 us
    pallas_call x1, Pallas kernels, local_fit(): pl.pallas_call(functools.partial(finish_kernel, fits), out_shape=(jax.Sha...  2.09 us

profile of v6, /device:TPU:97, one launch (start us, length us, event | category | flops | bytes accessed | tf_op | source)
XLA Modules:
  0.0 55.1 jit_solution(746198165939620757)
XLA Ops:
  0.6 52.2 %shard_map.67 = (f32[2,4096,128]{2,1,0:T(8,128)S(1)}, f32[8,2,8,128]{3,2,1,0:T(8,128)S(1)}) custom-call(f32[3]{0:T(128)} %beta_hbm.1, bf16[256,256]{1,0:T(8,128)(2,1)} %x_hbm.1, f32[2,4096,128]{2,1,0:T(8,128)} %mu_hbm.1, f32[2,4096]{1,0:T(2,128)} %logpi_hbm.1), custom_call_target="tpu_custom_call" | custom-call | tf_op jit(solution)/shard_map/pallas_call | solution.py:540
  52.8 2.1 %shard_map.68 = (f32[2,4096,128]{2,1,0:T(8,128)}, f32[2,4096]{1,0:T(2,128)}, f32[2,256]{1,0:T(2,128)}) custom-call(f32[2,4096,128]{2,1,0:T(8,128)S(1)} %get-tuple-element.5.mu_all, f32[8,2,8,128]{3,2,1,0:T(8,128)S(1)} %get-tuple-element.6.small), custom_call_target="tpu_custom_call" | custom-call | tf_op jit(solution)/shard_map/pallas_call | solution.py:580
